TPU v7x, 256 devices: a whole 4x4x8 slice. The times are simulated.
256 devices in a mesh: row: 8 (over z), col: 8 (over x_lo, y), layer: 4 (over x_hi, core).
Axes of the slice: x: 4 (x_hi: 2, x_lo: 2; x = x_hi * 2 + x_lo), y: 4, z: 8, core: 2. Of those that a mesh axis runs over, the one named last changes fastest.
Arguments:
- tokens: bfloat16 [5120, 6144], P('row', 'layer'), may hold values from -6 to 6
- expert_ids: int32 [5120, 2], replicated, may hold values from 0 to 7, all different within a row; in each aligned block of 5120 rows (0 to 5119, 5120 to 10239, ...) at most 2560 rows name the same one
- w_gate: bfloat16 [2, 6144, 8192], P(None, 'layer', ('row', 'col')), may hold values from -0.078125 to 0.078125
- w_up: bfloat16 [2, 6144, 8192], P(None, 'layer', ('row', 'col')), may hold values from -0.078125 to 0.078125
Outputs:
- hidden: bfloat16 [2, 2560, 8192], P(None, ('col', 'layer'), 'row')
Inputs may be any that keep to these rules, and one draw needn't show every extreme that they name: `expert_ids`: each token names 2 different experts. No expert is named by more than 2560 tokens, a bound that some block reaches.
All inputs are finite; a program needn't handle non-finite values.
Results may differ from a plain program's by a relative error of at most 0.0012.
Values may be sent and summed in bfloat16 or wider, within the bound.
A program may use at most 128 MiB of HBM per device.

v0:
```python
import jax
import jax.numpy as jnp
from jax import lax
from jax.sharding import PartitionSpec as P

SLOTS_DEV = 80


def laid_out(tiles, dim):
    tiles = jnp.moveaxis(tiles, 0, dim)
    shape = tiles.shape
    return tiles.reshape(*shape[:dim], shape[dim] * shape[dim + 1], *shape[dim + 2 :])


def on_gathered_pieces(x, axis, dim, apply, out_dim):
    size, span = (lax.axis_size(axis), x.shape[dim])
    count = 2 if span % 2 == 0 else 1
    done, length = ([], span // count)
    for k in range(count):
        piece = lax.slice_in_dim(x, k * length, (k + 1) * length, axis=dim)
        starts = jnp.arange(size) * span + k * length
        done.append(jax.vmap(apply)(lax.all_gather(piece, axis), starts))
    return laid_out(jnp.concatenate(done, axis=out_dim + 1), out_dim)


def shards(tokens, expert_ids, w_gate, w_up):
    col_count = lax.axis_size("col")
    layer_count = lax.axis_size("layer")
    row_count = lax.axis_size("row")
    col_index = lax.axis_index("col")
    row_index = lax.axis_index("row")
    experts = w_gate.shape[0]
    capacity = SLOTS_DEV * col_count * layer_count
    slot_block = capacity // col_count
    local_rows = tokens.shape[0]
    tok_count = local_rows * row_count
    expert_range = jnp.arange(experts, dtype=jnp.int32)
    member = jnp.any(expert_ids[:, :, None] == expert_range[None, None, :], axis=1).astype(
        jnp.int32
    )
    slot_rank = jnp.cumsum(member, axis=0) - member
    target = jnp.where(member > 0, slot_rank, capacity)
    token_range = jnp.broadcast_to(jnp.arange(tok_count, dtype=jnp.int32)[:, None], target.shape)
    slot_table = (
        jnp.zeros((experts, capacity + 1), jnp.int32)
        .at[expert_range[None, :], target]
        .set(token_range)
    )
    counts = jnp.sum(member, axis=0)
    slot_start = col_index * slot_block
    picked = lax.dynamic_slice_in_dim(slot_table, slot_start, slot_block, 1)
    position = slot_start + jnp.arange(slot_block, dtype=jnp.int32)
    live_mask = position[None, :] < counts[:, None]
    row_start = row_index * local_rows
    local_pick = picked - row_start
    inside = live_mask & (local_pick >= 0) & (local_pick < local_rows)
    own_rows = tokens[jnp.clip(local_pick, 0, local_rows - 1)]
    placed = jnp.where(inside[:, :, None], own_rows, jnp.zeros((), tokens.dtype)).astype(
        jnp.float32
    )
    slot_rows = lax.psum(placed.astype(jnp.bfloat16), "row")
    stacked = jnp.stack((w_gate, w_up))

    def project(piece, start):
        return jnp.einsum("ecd,pedf->pecf", slot_rows, piece, preferred_element_type=jnp.float32)

    totals = on_gathered_pieces(stacked, "col", 3, project, 3)
    parts = lax.psum_scatter(totals, "layer", scatter_dimension=2, tiled=True)
    return (jax.nn.silu(parts[0]) * parts[1]).astype(jnp.bfloat16)


def solution(mesh):
    in_specs = (
        P("row", "layer"),
        P(),
        P(None, "layer", ("row", "col")),
        P(None, "layer", ("row", "col")),
    )
    out_specs = P(None, ("col", "layer"), "row")
    return jax.shard_map(shards, mesh=mesh, in_specs=in_specs, out_specs=out_specs, check_vma=False)
```

profile of v0, /device:TPU:1, one launch (start us, length us, event | category | flops | bytes accessed | tf_op | source)
XLA Modules:
  0.0 269.2 jit_solution(11576271825753675574)
XLA Ops:
  7.4 0.0 copy-start
  7.4 0.0 all-gather.5.cloned.1.call-start
  7.4 1.5 copy.19
  8.9 1.4 copy.20
  10.3 0.0 copy-start.4
  10.3 0.0 copy-start.3
  10.4 1.3 fusion.10
  11.7 0.0 all-gather.5.cloned.1.call-update
  11.7 0.0 all-gather.7.cloned.1.call-start
  11.8 0.7 all-gather.7.cloned.1.call-update
  12.5 0.0 all-reduce.2.cloned.1.call-start
  12.5 0.9 compare_reduce_fusion
  13.4 0.6 reduce-window.6
  14.0 0.2 slice_reduce_fusion
  14.2 0.2 reduce-window.9
  14.4 0.1 add_bitcast_fusion
  14.5 0.2 convert_reduce_fusion
  14.7 0.0 copy-done.4
  14.7 0.1 multiply_reduce_fusion
  14.8 0.0 copy-done.3
  14.8 0.1 and_reduce_fusion
  15.0 2.3 copy.22
  17.3 3.1 %reshape.40 = s32[10240]{0:T(1024)S(1)} reshape(s32[5120,2]{1,0:T(8,128)} %copy.22) | data formatting | bytes 81920
  20.4 1.7 broadcast_in_dim.46
  22.1 3.1 %reshape.42 = s32[10240]{0:T(1024)S(1)} reshape(s32[5120,2]{1,0:T(8,128)} %broadcast_in_dim.46) | data formatting | bytes 81920 | tf_op jit(solution)/shard_map/broadcast_in_dim | solution.py:43
  25.2 38.0 %scatter_custom_fusion = s32[5122]{0:T(1024)S(1)} fusion(s32[10240]{0:T(1024)S(1)} %reshape.40, s32[10240]{0:T(1024)S(1)} %reshape.42, s32[]{:T(128)} %constant.16.clone.1), kind=kCustom, calls=%fused_computation.33 | custom fusion | bytes 20492
  63.1 0.1 reshape.30
  63.2 0.1 compare_select_fusion.2
  63.3 0.1 reshape.34
  63.4 0.0 copy-done
  63.4 3.7 %gather_fusion = bf16[640,1536]{1,0:T(8,128)(2,1)} fusion(bf16[640,1536]{1,0:T(8,128)(2,1)S(1)} %copy-done, s32[1024]{0:T(1024)S(1)} %pad_clamp_fusion), kind=kCustom, calls=%fused_computation | custom fusion | bytes 3934720 | tf_op jit(solution)/shard_map/gather | solution.py:57
  67.1 0.1 compare_and_fusion
  67.2 3.1 %broadcast_select_fusion = bf16[2,320,1536]{2,1,0:T(8,128)(2,1)} fusion(bf16[2,320,1536]{2,1,0:T(8,128)(2,1)} %bitcast.59, pred[2,320]{1,0:T(4,128)(4,1)S(1)} %compare_and_fusion), kind=kLoop, calls=%fused_computation.7 | loop fusion | flops 983040 | bytes 3932800 | tf_op jit(solution)/shard_map/jit(_where)/select_n | solution.py:58
  70.3 0.0 all-reduce.2.cloned.1.call-update
  70.3 0.2 reduce-scatter.2.cloned.1.call-start
  70.6 19.7 %all-gather.5.cloned.1.call-done = bf16[16,2,1536,64]{2,3,1,0:T(8,128)(2,1)} async-done(((bf16[2,2,1536,64]{2,3,1,0:T(8,128)(2,1)}), bf16[16,2,1536,64]{2,3,1,0:T(8,128)(2,1)}) %all-gather.5.cloned.1.call-update) | async-done | bytes 6291472 | tf_op jit(solution)/shard_map/all_gather | solution.py:22
  90.2 6.1 %copy.21 = bf16[16,2,1536,64]{2,3,0,1:T(8,128)(2,1)} copy(bf16[16,2,1536,64]{2,3,1,0:T(8,128)(2,1)} %all-gather.5.cloned.1.call-done) | data formatting | bytes 12582912 | tf_op jit(solution)/shard_map/all_gather | solution.py:22
  96.4 69.2 %all-gather.7.cloned.1.call-done = bf16[16,2,1536,64]{2,3,1,0:T(8,128)(2,1)} async-done(((bf16[2,2,1536,64]{2,3,1,0:T(8,128)(2,1)}), bf16[16,2,1536,64]{2,3,1,0:T(8,128)(2,1)}) %all-gather.7.cloned.1.call-update) | async-done | bytes 6291472 | tf_op jit(solution)/shard_map/all_gather | solution.py:22
  165.6 6.1 %copy.23 = bf16[16,2,1536,64]{2,3,0,1:T(8,128)(2,1)} copy(bf16[16,2,1536,64]{2,3,1,0:T(8,128)(2,1)} %all-gather.7.cloned.1.call-done) | data formatting | bytes 12582912 | tf_op jit(solution)/shard_map/all_gather | solution.py:22
  171.7 0.0 all-reduce.2.cloned.1.call-done
  171.7 0.0 copy-start.2
  171.7 0.0 copy-start.5
  171.7 6.3 %fusion.4 = f32[8,2,2,320,64]{3,4,1,0,2:T(8,128)S(1)} fusion(bf16[8,2,2,1536,64]{3,4,1,0,2:T(8,128)(2,1)} %bitcast.60, bf16[2,320,1536]{2,1,0:T(8,128)(2,1)} %all-reduce.2.cloned.1.call-done), kind=kOutput, calls=%fused_computation.8 | convolution fusion | flops 2013265920 | bytes 10878976 | tf_op jit(solution)/shard_map/vmap(ecd,pedf->pecf)/dot_general | solution.py:65
  178.0 0.0 copy-done.2
  178.0 0.0 copy-done.5
  178.0 3.4 %fusion.7 = f32[8,2,2,320,64]{3,4,1,0,2:T(8,128)S(1)} fusion(bf16[8,2,2,1536,64]{3,4,1,0,2:T(8,128)(2,1)S(1)} %bitcast.61, bf16[2,320,1536]{2,1,0:T(8,128)(2,1)S(1)} %copy-done.5), kind=kOutput, calls=%fused_computation.9 | convolution fusion | flops 2013265920 | bytes 10878976 | tf_op jit(solution)/shard_map/vmap(ecd,pedf->pecf)/dot_general | solution.py:65
  181.4 3.1 %maximum_bitcast_fusion = f32[2,2,320,8,128]{2,4,0,3,1:T(8,128)} fusion(f32[8,2,2,320,64]{3,4,1,0,2:T(8,128)S(1)} %fusion.7, f32[8,2,2,320,64]{3,4,1,0,2:T(8,128)S(1)} %fusion.4), kind=kLoop, calls=%fused_computation.2 | loop fusion | flops 1310720 | bytes 10485760 | tf_op jit(solution)/shard_map/transpose | solution.py:10
  184.5 6.3 %copy.24 = f32[2,2,320,8,128]{4,3,2,1,0:T(8,128)} copy(f32[2,2,320,8,128]{2,4,0,3,1:T(8,128)} %maximum_bitcast_fusion) | data formatting | bytes 10485760 | tf_op jit(solution)/shard_map/transpose | solution.py:10
  190.8 6.7 %reshape.26 = f32[2,2,320,1024]{3,2,1,0:T(8,128)} reshape(f32[2,2,320,8,128]{4,3,2,1,0:T(8,128)} %copy.24) | data formatting | bytes 10485760 | tf_op jit(solution)/shard_map/reshape | solution.py:12
  197.5 0.0 copy-start.1
  197.5 0.0 reduce-scatter.2.cloned.1.call-update
  197.6 62.0 %reduce-scatter.2.cloned.1.call-done = f32[2,2,80,1024]{3,2,1,0:T(8,128)} async-done(((f32[2,2,320,1024]{3,2,1,0:T(8,128)}), f32[2,2,80,1024]{3,2,1,0:T(8,128)}) %reduce-scatter.2.cloned.1.call-update) | async-done | bytes 1310736 | tf_op jit(solution)/shard_map/reduce_scatter | solution.py:68
  259.6 2.2 fusion.12
  261.8 0.0 copy-done.1
  (6 shorter events, 0.1 us)
Async XLA Ops:
  7.4 56.0 %copy-start = (bf16[640,1536]{1,0:T(8,128)(2,1)S(1)}, bf16[640,1536]{1,0:T(8,128)(2,1)}, u32[]{:S(2)}) copy-start(bf16[640,1536]{1,0:T(8,128)(2,1)} %param.4) | copy-start | bytes 5898244
  7.4 82.9 %all-gather.5.cloned.1.call-start = ((), (), s32[]{:S(2)}) async-start(), calls=%async_computation.3 | async-start | bytes 7077888 | tf_op jit(solution)/shard_map/all_gather | solution.py:22
  10.3 4.4 %copy-start.4 = (s32[2]{0:T(128)S(1)}, s32[2]{0:T(128)}, u32[]{:S(2)}) copy-start(s32[2]{0:T(128)} %constant.40) | copy-start | bytes 28
  10.3 4.5 %copy-start.3 = (s32[2]{0:T(128)S(1)}, s32[2]{0:T(128)}, u32[]{:S(2)}) copy-start(s32[2]{0:T(128)} %constant.43) | copy-start | bytes 28
  11.7 153.9 %all-gather.7.cloned.1.call-start = ((), (), s32[]{:S(2)}) async-start(), calls=%async_computation.4 | async-start | bytes 7077888 | tf_op jit(solution)/shard_map/all_gather | solution.py:22
  12.5 159.2 %all-reduce.2.cloned.1.call-start = ((), (), s32[]{:S(2)}) async-start(), calls=%async_computation.1 | async-start | bytes 3932160 | tf_op jit(solution)/shard_map/psum | solution.py:61
  70.3 189.3 %reduce-scatter.2.cloned.1.call-start = ((), (), s32[]{:S(2)}) async-start(), calls=%async_computation.2 | async-start | bytes 6553600 | tf_op jit(solution)/shard_map/reduce_scatter | solution.py:68
  171.7 6.3 %copy-start.2 = (bf16[16,2,1536,64]{2,3,0,1:T(8,128)(2,1)S(1)}, bf16[16,2,1536,64]{2,3,0,1:T(8,128)(2,1)}, u32[]{:S(2)}) copy-start(bf16[16,2,1536,64]{2,3,0,1:T(8,128)(2,1)} %copy.23) | copy-start | bytes 18874372
  171.7 6.3 %copy-start.5 = (bf16[2,320,1536]{2,1,0:T(8,128)(2,1)S(1)}, bf16[2,320,1536]{2,1,0:T(8,128)(2,1)}, u32[]{:S(2)}) copy-start(bf16[2,320,1536]{2,1,0:T(8,128)(2,1)} %all-reduce.2.cloned.1.call-done) | copy-start | bytes 5898244
  197.5 64.2 %copy-start.1 = (bf16[640,1536]{1,0:T(8,128)(2,1)S(1)}, bf16[640,1536]{1,0:T(8,128)(2,1)}, u32[]{:S(2)}) copy-start(bf16[640,1536]{1,0:T(8,128)(2,1)} %param.4) | copy-start | bytes 5898244
Sparse Core Ops, SparseCore 0:
  11.8 78.3 all-gather.4
  92.0 73.5 all-gather.6
Sparse Core Ops, SparseCore 1:
  70.4 81.0 all-reduce.1
  197.6 61.9 reduce-scatter.1
where the time goes:
time: 270 us; the launch traced here: 269 us
  waiting for transfers between devices  152 us (56%)
  local copies, waits for them, and re-layouts  80.4 us (30%)
  between operations  15 us (6%)
  other arithmetic  12.1 us (4%)
  matrix products  9.66 us (4%)
    all_gather x2, waiting for transfers between devices, on_gathered_pieces(): done.append(jax.vmap(apply)(lax.all_gather(piece, axis), starts))  88.9 us
    reduce_scatter x1, waiting for transfers between devices, shards(): parts = lax.psum_scatter(totals, 'layer', scatter_dimension=2, tiled=True)  62 us
    unnamed x18, local copies, waits for them, and re-layouts  46.3 us
    all_gather x2, local copies, waits for them, and re-layouts, on_gathered_pieces(): done.append(jax.vmap(apply)(lax.all_gather(piece, axis), starts))  12.2 us
    dot_general x2, matrix products, project(): jnp.einsum('ecd,pedf->pecf', slot_rows, piece, preferred_element_type=jnp...  9.66 us
    reshape x1, local copies, waits for them, and re-layouts, laid_out(): tiles.reshape(*shape[:dim], shape[dim] * shape[dim + 1], *shape[dim + 2:])  6.73 us
    transpose x1, local copies, waits for them, and re-layouts, laid_out(): tiles = jnp.moveaxis(tiles, 0, dim)  6.3 us
  transfers between devices with their start and end apart: 4, of which 3 were waited for; matrix products, arithmetic and copies ran while one was open for 26% of the time, Pallas kernels for 0%

commit v1 on v0

v1 whole, which is shorter than its diff:
```python
import functools

import jax
import jax.numpy as jnp
from jax import lax
from jax.experimental import pallas as pl
from jax.experimental.pallas import tpu as pltpu
from jax.sharding import PartitionSpec as P

MESH = pl.DeviceIdType.MESH
ROWS = 8
BLOCK = 80
HALF = 768
LANES = 128
EXPERTS = 2


def ring_steps(first):
    return (4, 3) if first else (3, 4)


def kernel(
    rank_ref, tok_ref, wg_ref, wu_ref, out_ref,
    wbuf, placed, sums, slots, part, from_core, from_hi, sent, back,
    w_s, w_r, rs_s, rs_r, x_s, x_r, ag_s, ag_r, c_s, c_r, h_s, h_r, o_s, o_r,
):
    z = lax.axis_index("row")
    col = lax.axis_index("col")
    layer = lax.axis_index("layer")
    xl, y = col // 4, col % 4
    xh, core = layer // 2, layer % 2

    def at_row(step):
        return (lax.rem(z + step + ROWS, ROWS), col, layer)

    def at_y(step):
        return (z, xl * 4 + lax.rem(y + step, 4), layer)

    pair = (z, (1 - xl) * 4 + y, layer)
    other_core = (z, col, xh * 2 + (1 - core))
    other_hi = (z, col, (1 - xh) * 2 + core)
    y_steps = (1, 3, 2)

    barrier = pltpu.get_barrier_semaphore()
    partners = [at_row(1), at_row(-1), at_y(1), at_y(2), at_y(3), pair, other_core, other_hi]
    for partner in partners:
        pl.semaphore_signal(barrier, inc=1, device_id=partner, device_id_type=MESH)
    pl.semaphore_wait(barrier, len(partners))

    pending = []

    def send(src, dst, send_sem, recv_sem, device):
        copy = pltpu.make_async_remote_copy(
            src_ref=src, dst_ref=dst, send_sem=send_sem, recv_sem=recv_sem,
            device_id=device, device_id_type=MESH,
        )
        copy.start()
        pending.append(copy)
        return copy

    w_copies = {}

    def send_weights(e):
        for d, step in enumerate(y_steps):
            for g, ref in enumerate((wg_ref, wu_ref)):
                w_copies[e, d, g] = send(
                    ref.at[e], wbuf.at[y, e, :, pl.ds(g * LANES, LANES)],
                    w_s.at[e, d, g], w_r.at[e, d, g], at_y(step),
                )

    send_weights(0)

    rs_copies = {}

    def owner_rows(ref, e, k):
        start = pl.multiple_of((k // 2) * BLOCK, 16)
        return ref.at[e, k % 2, pl.ds(start, BLOCK), :]

    def reduce_step(e, s):
        for d, sign in enumerate((1, -1)):
            steps = ring_steps(e == 0)[d]
            if s > steps:
                continue
            k = lax.rem(z + sign * (steps - s + 1) + ROWS, ROWS)
            if s == 1:
                src = owner_rows(placed, e, k)
            else:
                rs_copies[e, d, s - 1].wait_recv()
                src = sums.at[e, d, s - 2]
                src[...] = src[...] + owner_rows(placed, e, k)[...]
            rs_copies[e, d, s] = send(
                src, sums.at[e, d, s - 1], rs_s.at[e, d, s - 1], rs_r.at[e, d, s - 1], at_row(sign)
            )

    for e in range(EXPERTS):
        base = col * (4 * BLOCK)
        place = lax.broadcasted_iota(jnp.int32, (4 * BLOCK, tok_ref.shape[0]), 0) + base
        pick = (place == rank_ref[pl.ds(e, 1), :]).astype(jnp.float32).astype(jnp.bfloat16)
        for f in range(2):
            placed[e, f] = jnp.dot(
                pick, tok_ref[:, f * HALF : (f + 1) * HALF], preferred_element_type=jnp.float32
            ).astype(jnp.bfloat16)
        reduce_step(e, 1)

    for e in range(EXPERTS):
        wbuf[y, e, :, 0:LANES] = wg_ref[e]
        wbuf[y, e, :, LANES : 2 * LANES] = wu_ref[e]

    for s in range(2, 5):
        for e in range(EXPERTS):
            reduce_step(e, s)

    def slot_rows(e, k, half):
        start = pl.multiple_of((k // 2) * (2 * BLOCK) + half * BLOCK, 16)
        return slots.at[e, k % 2, pl.ds(start, BLOCK), :]

    x_copies = {}

    def finish_reduce(e):
        up, down = ring_steps(e == 0)
        rs_copies[e, 0, up].wait_recv()
        rs_copies[e, 1, down].wait_recv()
        total = sums[e, 0, up - 1] + sums[e, 1, down - 1] + owner_rows(placed, e, z)[...]
        mine = slot_rows(e, z, xl)
        mine[...] = total
        x_copies[e] = send(mine, mine, x_s.at[e], x_r.at[e], pair)

    ag_copies = {}

    def gather_step(e, h, s):
        half = xl if h == 0 else 1 - xl
        for d, sign in enumerate((1, -1)):
            if s > ring_steps(h == 0)[d]:
                continue
            k = lax.rem(z - sign * (s - 1) + ROWS, ROWS)
            if s > 1:
                ag_copies[e, h, d, s - 1].wait_recv()
            rows = slot_rows(e, k, half)
            ag_copies[e, h, d, s] = send(
                rows, rows, ag_s.at[e, h, d, s - 1], ag_r.at[e, h, d, s - 1], at_row(sign)
            )

    def gather_done(e):
        for h in range(2):
            for d in range(2):
                ag_copies[e, h, d, ring_steps(h == 0)[d]].wait_recv()

    def project(e):
        @pl.loop(0, 4)
        def _(b):
            total = jnp.dot(
                slots[e, 0], wbuf[b, e, 0:HALF, :], preferred_element_type=jnp.float32
            ) + jnp.dot(
                slots[e, 1], wbuf[b, e, HALF : 2 * HALF, :], preferred_element_type=jnp.float32
            )
            for a in range(4):
                for side in range(2):
                    start = (a * 2 + side) * BLOCK
                    part[e, a % 2, a // 2, side, b] = total[start : start + BLOCK]

    c_copies, h_copies, o_copies = {}, {}, {}

    def to_core(e):
        for i, hi in enumerate((1 - xh, xh)):
            c_copies[e, i] = send(
                part.at[e, 1 - core, hi], from_core.at[e, hi], c_s.at[e, i], c_r.at[e, i], other_core
            )

    def to_hi(e):
        c_copies[e, 0].wait_recv()
        src = part.at[e, core, 1 - xh]
        for side in range(2):
            for b in range(4):
                src[side, b] = src[side, b] + from_core[e, 1 - xh, side, b]
        h_copies[e] = send(src, from_hi.at[e], h_s.at[e], h_r.at[e], other_hi)

    def finish(e):
        c_copies[e, 1].wait_recv()
        h_copies[e].wait_recv()

        def hidden(side, b):
            total = part[e, core, xh, side, b] + from_core[e, xh, side, b] + from_hi[e, side, b]
            gate, up = total[:, :LANES], total[:, LANES:]
            return (gate / (1.0 + jnp.exp(-gate)) * up).astype(jnp.bfloat16)

        for b in range(4):
            sent[e, :, b * LANES : (b + 1) * LANES] = hidden(1 - xl, b)
        o_copies[e] = send(sent.at[e], back.at[e], o_s.at[e], o_r.at[e], pair)
        for b in range(4):
            start = pl.multiple_of((xl * 4 + b) * LANES, LANES)
            out_ref[e, :, pl.ds(start, LANES)] = hidden(xl, b)

    def weights_done(e):
        for d in range(3):
            for g in range(2):
                w_copies[e, d, g].wait_recv()

    finish_reduce(0)
    gather_step(0, 0, 1)
    send_weights(1)
    finish_reduce(1)
    x_copies[0].wait_recv()
    gather_step(0, 1, 1)
    for s in (2, 3):
        gather_step(0, 0, s)
        gather_step(0, 1, s)
    gather_step(1, 0, 1)
    x_copies[1].wait_recv()
    gather_step(1, 1, 1)
    gather_step(0, 0, 4)
    gather_step(0, 1, 4)
    gather_step(1, 0, 2)
    gather_step(1, 1, 2)
    gather_done(0)
    weights_done(0)
    project(0)
    to_core(0)
    gather_step(1, 0, 3)
    gather_step(1, 1, 3)
    to_hi(0)
    gather_step(1, 0, 4)
    gather_step(1, 1, 4)
    gather_done(1)
    weights_done(1)
    project(1)
    to_core(1)
    to_hi(1)
    finish(0)
    finish(1)
    for e in range(EXPERTS):
        o_copies[e].wait_recv()
        start = pl.multiple_of((1 - xl) * 4 * LANES, LANES)
        out_ref[e, :, pl.ds(start, 4 * LANES)] = back[e]
    for copy in pending:
        copy.wait_send()


def ranks(expert_ids, rows):
    tokens = expert_ids.shape[0]
    ids = expert_ids.T.reshape(2, tokens // LANES, LANES)
    experts = jnp.arange(EXPERTS, dtype=jnp.int32)[:, None, None]
    member = (ids[0][None] == experts) | (ids[1][None] == experts)
    ones = member.astype(jnp.bfloat16)
    lane = jnp.arange(LANES)
    before = (lane[:, None] < lane[None, :]).astype(jnp.bfloat16)
    within = jnp.einsum("erk,kl->erl", ones, before, preferred_element_type=jnp.float32)
    counts = jnp.sum(member.astype(jnp.float32), axis=2)
    line = jnp.arange(tokens // LANES)
    ahead = jnp.sum(jnp.where(line[None, :, None] > line[None, None, :], counts[:, None, :], 0.0), axis=2)
    rank = jnp.where(member, (within + ahead[:, :, None]).astype(jnp.int32), -1)
    start = lax.axis_index("row") * (rows // LANES)
    return lax.dynamic_slice_in_dim(rank, start, rows // LANES, 1).reshape(EXPERTS, rows)


def shards(tokens, expert_ids, w_gate, w_up):
    rank = ranks(expert_ids, tokens.shape[0])
    bf16, f32 = jnp.bfloat16, jnp.float32
    vmem, dma = pltpu.VMEM, pltpu.SemaphoreType.DMA
    return pl.pallas_call(
        kernel,
        name="experts",
        out_shape=jax.ShapeDtypeStruct((EXPERTS, BLOCK, 1024), bf16),
        in_specs=[pl.BlockSpec(memory_space=pltpu.VMEM)] * 4,
        out_specs=pl.BlockSpec(memory_space=pltpu.VMEM),
        scratch_shapes=[
            vmem((4, EXPERTS, 2 * HALF, 2 * LANES), bf16),
            vmem((EXPERTS, 2, 4 * BLOCK, HALF), bf16),
            vmem((EXPERTS, 2, 4, BLOCK, HALF), bf16),
            vmem((EXPERTS, 2, 8 * BLOCK, HALF), bf16),
            vmem((EXPERTS, 2, 2, 2, 4, BLOCK, 2 * LANES), f32),
            vmem((EXPERTS, 2, 2, 4, BLOCK, 2 * LANES), f32),
            vmem((EXPERTS, 2, 4, BLOCK, 2 * LANES), f32),
            vmem((EXPERTS, BLOCK, 4 * LANES), bf16),
            vmem((EXPERTS, BLOCK, 4 * LANES), bf16),
            dma((EXPERTS, 3, 2)), dma((EXPERTS, 3, 2)),
            dma((EXPERTS, 2, 4)), dma((EXPERTS, 2, 4)),
            dma((EXPERTS,)), dma((EXPERTS,)),
            dma((EXPERTS, 2, 2, 4)), dma((EXPERTS, 2, 2, 4)),
            dma((EXPERTS, 2)), dma((EXPERTS, 2)),
            dma((EXPERTS,)), dma((EXPERTS,)),
            dma((EXPERTS,)), dma((EXPERTS,)),
        ],
        compiler_params=pltpu.CompilerParams(
            collective_id=0, has_side_effects=True, vmem_limit_bytes=60 * 1024 * 1024
        ),
    )(rank, tokens, w_gate, w_up)


def solution(mesh):
    in_specs = (
        P("row", "layer"),
        P(),
        P(None, "layer", ("row", "col")),
        P(None, "layer", ("row", "col")),
    )
    out_specs = P(None, ("col", "layer"), "row")
    return jax.shard_map(shards, mesh=mesh, in_specs=in_specs, out_specs=out_specs, check_vma=False)
```

time: 270 us -> 111 us (0.41)
  waiting for transfers between devices: 152 us -> 0 us
  Pallas kernels: 0 us -> 107 us
  local copies, waits for them, and re-layouts: 80.4 us -> 3.29 us
  between operations: 15 us -> 0.02 us
  other arithmetic: 12.1 us -> 0.27 us
  matrix products: 9.66 us -> 0.14 us
    pallas_call x0 -> x1, Pallas kernels: none -> 107 us  [shards(): pl.pallas_call(kernel, name='experts', out_shape=jax.ShapeDtypeStruct((EX...]
    all_gather x2 -> x0, waiting for transfers between devices: 88.9 us -> none  [on_gathered_pieces(): done.append(jax.vmap(apply)(lax.all_gather(piece, axis), starts))]
    reduce_scatter x1 -> x0, waiting for transfers between devices: 62 us -> none  [shards(): parts = lax.psum_scatter(totals, 'layer', scatter_dimension=2, tiled=True)]
    unnamed x18 -> x2, local copies, waits for them, and re-layouts: 46.3 us -> 2.32 us
    all_gather x2 -> x0, local copies, waits for them, and re-layouts: 12.2 us -> none  [on_gathered_pieces(): done.append(jax.vmap(apply)(lax.all_gather(piece, axis), starts))]
    dot_general x2 -> x1, matrix products: 9.66 us -> 0.14 us  [ranks(): jnp.einsum('erk,kl->erl', ones, before, preferred_element_type=jnp.float32)]
    reshape x1 -> x0, local copies, waits for them, and re-layouts: 6.73 us -> none  [laid_out(): tiles.reshape(*shape[:dim], shape[dim] * shape[dim + 1], *shape[dim + 2:])]
    transpose x1 -> x0, local copies, waits for them, and re-layouts: 6.3 us -> none  [laid_out(): tiles = jnp.moveaxis(tiles, 0, dim)]
  transfers between devices with their start and end apart: 4 -> 0, of which waited for: 3 -> 0; matrix products, arithmetic and copies ran while one was open for 26% -> 0% of each run, Pallas kernels for 0% -> 0%
where the time goes in v1:
time: 111 us
  Pallas kernels  107 us (96%)
  local copies, waits for them, and re-layouts  3.29 us (3%)
    pallas_call x1, Pallas kernels, shards(): pl.pallas_call(kernel, name='experts', out_shape=jax.ShapeDtypeStruct((EX...  107 us
    unnamed x2, local copies, waits for them, and re-layouts  2.32 us

profile of v1, /device:TPU:1, one launch (start us, length us, event | category | flops | bytes accessed | tf_op | source)
XLA Modules:
  0.0 110.5 jit_solution(10526344658303246842)
XLA Ops:
  0.0 0.9 fusion.8
  0.9 0.1 convert_reduce_fusion
  1.0 0.1 select_reduce_fusion
  1.1 0.1 constant_dynamic-slice_fusion
  1.2 0.1 fusion.1
  1.3 0.1 fusion.6
  1.4 0.6 copy.7
  2.0 106.8 %experts.1 = bf16[2,80,1024]{2,1,0:T(8,128)(2,1)} custom-call(s32[2,640]{1,0:T(2,128)} %bitcast.15, bf16[640,1536]{1,0:T(8,128)(2,1)} %tok_ref.1, bf16[2,1536,128]{2,1,0:T(8,128)(2,1)} %wg_ref.1, bf16[2,1536,128]{2,1,0:T(8,128)(2,1)} %wu_ref.1), custom_call_target="tpu_custom_call" | custom-call | tf_op jit(solution)/shard_map/experts/pallas_call | solution.py:259
  108.8 1.7 %copy.9 = bf16[2,80,1024]{2,1,0:T(8,128)(2,1)} copy(bf16[2,80,1024]{2,1,0:T(8,128)(2,1)} %experts.1) | data formatting | bytes 655360
  (1 shorter events, 0.0 us)

commit v2 on v0

v2 whole, which is shorter than its diff:
```python
import jax
import jax.numpy as jnp
from jax import lax
from jax.experimental import pallas as pl
from jax.experimental.pallas import tpu as pltpu
from jax.sharding import PartitionSpec as P

MESH = pl.DeviceIdType.MESH
ROWS = 8
BLOCK = 80
DEPTH = 1536
QUARTER = DEPTH // 4
HALF = DEPTH // 2
LANES = 128
EXPERTS = 2
CHUNKS = ((0, 0), (1, 0), (0, 1), (1, 1))
SIDEWAYS = (0,)
Y_STEP = (0, 1, 3, 2)
PIECES = ((0, 3), (3, 1))


def ring_steps(odd):
    return (3, 4) if odd else (4, 3)


class Copy:
    def __init__(self, src, dst, send_sem, recv_sem, device):
        self.copy = pltpu.make_async_remote_copy(
            src_ref=src, dst_ref=dst, send_sem=send_sem, recv_sem=recv_sem,
            device_id=device, device_id_type=MESH,
        )
        self.copy.start()
        self.arrived = False

    def wait(self):
        if not self.arrived:
            self.copy.wait_recv()
        self.arrived = True


def kernel(
    ids_ref, tok_ref, wg_ref, wu_ref, out_ref,
    wbuf, placed, sums, slots, part, from_core, from_hi, sent, back,
    w_s, w_r, wf_s, wf_r, rs_s, rs_r, x_s, x_r, ag_s, ag_r, c_s, c_r, h_s, h_r, o_s, o_r,
):
    z = lax.axis_index("row")
    col = lax.axis_index("col")
    layer = lax.axis_index("layer")
    xl, y = col // 4, col % 4
    xh, core = layer // 2, layer % 2

    def at_row(step):
        return (lax.rem(z + step + ROWS, ROWS), col, layer)

    def at_y(step):
        return (z, xl * 4 + lax.rem(y + step, 4), layer)

    pair = (z, (1 - xl) * 4 + y, layer)
    other_core = (z, col, xh * 2 + (1 - core))
    other_hi = (z, col, (1 - xh) * 2 + core)

    barrier = pltpu.get_barrier_semaphore()
    partners = [at_row(1), at_row(-1), at_y(1), at_y(3), pair, other_core, other_hi]
    for partner in partners:
        pl.semaphore_signal(barrier, inc=1, device_id=partner, device_id_type=MESH)
    pl.semaphore_wait(barrier, len(partners))

    copies = {}

    def send(key, src, dst, send_sem, recv_sem, device):
        copies[key] = Copy(src, dst, send_sem, recv_sem, device)

    def send_weights(e):
        for i in range(2):
            for d in range(2):
                half = i if d == 0 else 1 - i
                rows = pl.ds(half * HALF, HALF)
                for g, ref in enumerate((wg_ref, wu_ref)):
                    send(
                        ("w", e, d, half, g), ref.at[e, rows, :],
                        wbuf.at[2 - d, e, rows, pl.ds(g * LANES, LANES)],
                        w_s.at[e, d, half, g], w_r.at[e, d, half, g], at_y(1 if d == 0 else 3),
                    )

    def pass_weights(e):
        for d in range(2):
            for g in range(2):
                copies["w", e, d, d, g].wait()
            rows = pl.ds(d * HALF, HALF)
            send(
                ("f", e, d), wbuf.at[2 - d, e, rows, :], wbuf.at[3, e, rows, :],
                wf_s.at[e, d], wf_r.at[e, d], at_y(1 if d == 0 else 3),
            )

    def own_weights(e):
        wbuf[0, e, :, 0:LANES] = wg_ref[e]
        wbuf[0, e, :, LANES : 2 * LANES] = wu_ref[e]

    def weights_done(e, piece):
        if piece == 0:
            for d in range(2):
                for half in range(2):
                    for g in range(2):
                        copies["w", e, d, half, g].wait()
        else:
            for d in range(2):
                copies["f", e, d].wait()

    count = tok_ref.shape[0]
    start = pl.multiple_of(z * count, LANES)
    rank = []

    def find_ranks():
        above = lax.broadcasted_iota(jnp.int32, (count, count), 0)
        right = lax.broadcasted_iota(jnp.int32, (count, count), 1)
        before = (above < right).astype(jnp.float32).astype(jnp.bfloat16)
        token = lax.broadcasted_iota(jnp.int32, (1, ids_ref.shape[1]), 1)
        for e in range(EXPERTS):
            named = (ids_ref[0:1, :] == e) | (ids_ref[1:2, :] == e)
            ahead = jnp.sum((named & (token < start)).astype(jnp.float32), axis=1, keepdims=True)
            here = pl.ds(start, count)
            own = (ids_ref[0:1, here] == e) | (ids_ref[1:2, here] == e)
            ones = jnp.broadcast_to(own.astype(jnp.float32), (16, count)).astype(jnp.bfloat16)
            within = jnp.dot(ones, before, preferred_element_type=jnp.float32)[0:1]
            rank.append(jnp.where(own, (within + ahead).astype(jnp.int32), -1))

    def slot_start(c, r):
        to_hi = xh if CHUNKS[c][1] else 1 - xh
        to_core = core if r else 1 - core
        return (col * 4 + to_hi * 2 + to_core) * BLOCK

    def place_rows(c):
        index = lax.broadcasted_iota(jnp.int32, (BLOCK, count), 0)
        slot = jnp.concatenate([index + slot_start(c, 0), index + slot_start(c, 1)], axis=0)
        pick = (slot == rank[CHUNKS[c][0]]).astype(jnp.float32).astype(jnp.bfloat16)
        for f in range(2):
            placed[c, :, f * HALF : (f + 1) * HALF] = jnp.dot(
                pick, tok_ref[:, f * HALF : (f + 1) * HALF], preferred_element_type=jnp.float32
            ).astype(jnp.bfloat16)

    def owner_lanes(k):
        return pl.ds(pl.multiple_of((k % 4) * QUARTER, LANES), QUARTER)

    def owner_rows(c, k):
        return placed.at[c, pl.ds(pl.multiple_of((k // 4) * BLOCK, 16), BLOCK), owner_lanes(k)]

    def reduce_step(c, s):
        for d, sign in enumerate((1, -1)):
            steps = ring_steps(c % 2)[d]
            if s > steps:
                continue
            k = lax.rem(z + sign * (steps - s + 1) + ROWS, ROWS)
            if s == 1:
                src = owner_rows(c, k)
            else:
                copies["r", c, d, s - 1].wait()
                src = sums.at[c, d, s - 2]
                src[...] = src[...] + owner_rows(c, k)[...]
            send(
                ("r", c, d, s), src, sums.at[c, d, s - 1],
                rs_s.at[c, d, s - 1], rs_r.at[c, d, s - 1], at_row(sign),
            )

    def slot_rows(c, k, side):
        first = pl.multiple_of((k // 4) * (2 * BLOCK) + side * BLOCK, 16)
        return slots.at[c, pl.ds(first, BLOCK), owner_lanes(k)]

    def both_sides(c, k):
        first = pl.multiple_of((k // 4) * (2 * BLOCK), 16)
        return slots.at[c, pl.ds(first, 2 * BLOCK), owner_lanes(k)]

    def to_pair(c, i, k):
        rows = slot_rows(c, k, xl)
        send(("x", c, i), rows, rows, x_s.at[c, i], x_r.at[c, i], pair)

    def finish_reduce(c):
        up, down = ring_steps(c % 2)
        copies["r", c, 0, up].wait()
        copies["r", c, 1, down].wait()
        mine = slot_rows(c, z, xl)
        mine[...] = sums[c, 0, up - 1] + sums[c, 1, down - 1] + owner_rows(c, z)[...]
        if c in SIDEWAYS:
            gather_step(c, 1)
        else:
            to_pair(c, 0, z)

    def gather_step(c, s):
        if s == 1:
            if c in SIDEWAYS:
                to_pair(c, 0, z)
            else:
                copies["x", c, 0].wait()
        for d, sign in enumerate((1, -1)):
            steps = ring_steps(1 - c % 2)[d]
            if s - 1 > steps:
                continue
            k = lax.rem(z - sign * (s - 1) + ROWS, ROWS)
            if s > 1:
                copies["a", c, d, s - 1].wait()
            if s <= steps:
                rows = slot_rows(c, k, xl) if c in SIDEWAYS else both_sides(c, k)
                send(
                    ("a", c, d, s), rows, rows,
                    ag_s.at[c, d, s - 1], ag_r.at[c, d, s - 1], at_row(sign),
                )
            if s > 1 and c in SIDEWAYS:
                to_pair(c, 1 + d * ring_steps(1 - c % 2)[0] + s - 2, k)

    def slots_done(c):
        gather_step(c, 5)
        if c in SIDEWAYS:
            for i in range(8):
                copies["x", c, i].wait()

    def project(c, piece, r=None):
        e = CHUNKS[c][0]
        first, number = PIECES[piece]
        rows = range(2) if r is None else (r,)
        top = rows[0] * 2 * BLOCK
        span = len(rows) * 2 * BLOCK

        @pl.loop(first, first + number)
        def _(b):
            total = jnp.dot(
                slots[c, top : top + span, :], wbuf[b, e], preferred_element_type=jnp.float32
            )
            for i, row in enumerate(rows):
                for side in range(2):
                    at = (i * 2 + side) * BLOCK
                    part[c, row, b, side] = total[at : at + BLOCK]

    def to_core(c, piece):
        here = pl.ds(*PIECES[piece])
        send(
            ("c", c, piece), part.at[c, 0, here], from_core.at[c, here],
            c_s.at[c, piece], c_r.at[c, piece], other_core,
        )

    def to_hi(c, piece):
        e = CHUNKS[c][0]
        first, number = PIECES[piece]
        copies["c", c, piece].wait()

        @pl.loop(first, first + number)
        def _(b):
            for side in range(2):
                part[c, 1, b, side] = part[c, 1, b, side] + from_core[c, b, side]

        here = pl.ds(first, number)
        send(
            ("h", e, piece), part.at[c, 1, here], from_hi.at[e, here],
            h_s.at[e, piece], h_r.at[e, piece], other_hi,
        )

    def finish(e):
        c = CHUNKS.index((e, 1))
        for piece in range(2):
            copies["h", e, piece].wait()
        for piece in range(2):
            copies["c", c, piece].wait()

        def hidden(side, b):
            total = part[c, 1, b, side] + from_core[c, b, side] + from_hi[e, b, side]
            gate, up = total[:, :LANES], total[:, LANES:]
            return (gate / (1.0 + jnp.exp(-gate)) * up).astype(jnp.bfloat16)

        for b in range(4):
            sent[e, :, b * LANES : (b + 1) * LANES] = hidden(1 - xl, b)
        send(("o", e), sent.at[e], back.at[e], o_s.at[e], o_r.at[e], pair)
        for b in range(4):
            out_ref[e, :, out_lanes(xl, b)] = hidden(xl, b)

    def out_lanes(side, b):
        return pl.ds(pl.multiple_of((side * 4 + lax.rem(y + Y_STEP[b], 4)) * LANES, LANES), LANES)

    def take_back(e):
        copies["o", e].wait()
        for b in range(4):
            out_ref[e, :, out_lanes(1 - xl, b)] = back[e, :, b * LANES : (b + 1) * LANES]

    def project_all(c):
        for piece in range(2):
            weights_done(CHUNKS[c][0], piece)
            project(c, piece)
            to_core(c, piece)

    def project_rows(c):
        for piece in range(2):
            weights_done(CHUNKS[c][0], piece)
        for r in range(2):
            for piece in range(2):
                project(c, piece, r)
                if r == 0:
                    to_core(c, piece)

    plan = [
        (0.0, send_weights, 0),
        (0.1, find_ranks),
        (2.2, own_weights, 0),
        (4.4, own_weights, 1),
        (10.5, pass_weights, 0),
        (13.0, send_weights, 1),
        (37.0, pass_weights, 1),
    ]
    first_reduce = (1.0, 1.5, 9.0, 15.0)
    reduce_gap = (3.2, 3.2, 3.2, 3.2)
    first_gather = (14.5, 18.0, 31.0, 40.0)
    gather_gap = (3.2, 4.4, 4.4, 4.4)
    for c in range(4):
        plan.append((first_reduce[c] - 0.1, place_rows, c))
        for s in range(1, 5):
            plan.append((first_reduce[c] + (s - 1) * reduce_gap[c], reduce_step, c, s))
        plan.append((first_reduce[c] + 4 * reduce_gap[c], finish_reduce, c))
        for s in range(1 + (c in SIDEWAYS), 5):
            plan.append((first_gather[c] + (s - 1) * gather_gap[c], gather_step, c, s))
    plan += [
        (31.0, slots_done, 0), (31.1, project_all, 0), (34.0, to_hi, 0, 0), (34.5, to_hi, 0, 1),
        (38.0, slots_done, 1), (43.0, weights_done, 1, 0), (43.1, project, 1, 0), (43.2, to_core, 1, 0),
        (46.0, to_hi, 1, 0),
        (50.0, slots_done, 2), (50.1, project_all, 2),
        (51.0, weights_done, 1, 1), (51.1, project, 1, 1), (51.2, to_core, 1, 1), (52.5, to_hi, 1, 1),
        (55.0, finish, 0),
        (59.0, slots_done, 3), (59.1, project_rows, 3), (62.0, finish, 1),
        (64.0, take_back, 0), (65.0, take_back, 1),
    ]
    for _, act, *args in sorted(plan, key=lambda step: step[0]):
        act(*args)
    for copy in copies.values():
        copy.copy.wait_send()


def shards(tokens, expert_ids, w_gate, w_up):
    bf16, f32 = jnp.bfloat16, jnp.float32
    vmem, dma = pltpu.VMEM, pltpu.SemaphoreType.DMA
    chunks = len(CHUNKS)
    return pl.pallas_call(
        kernel,
        name="experts",
        out_shape=jax.ShapeDtypeStruct((EXPERTS, BLOCK, 1024), bf16),
        in_specs=[pl.BlockSpec(memory_space=pltpu.VMEM)] * 4,
        out_specs=pl.BlockSpec(memory_space=pltpu.VMEM),
        scratch_shapes=[
            vmem((4, EXPERTS, DEPTH, 2 * LANES), bf16),
            vmem((chunks, 2 * BLOCK, DEPTH), bf16),
            vmem((chunks, 2, 4, BLOCK, QUARTER), bf16),
            vmem((chunks, 4 * BLOCK, DEPTH), bf16),
            vmem((chunks, 2, 4, 2, BLOCK, 2 * LANES), f32),
            vmem((chunks, 4, 2, BLOCK, 2 * LANES), f32),
            vmem((EXPERTS, 4, 2, BLOCK, 2 * LANES), f32),
            vmem((EXPERTS, BLOCK, 4 * LANES), bf16),
            vmem((EXPERTS, BLOCK, 4 * LANES), bf16),
            dma((EXPERTS, 2, 2, 2)), dma((EXPERTS, 2, 2, 2)),
            dma((EXPERTS, 2)), dma((EXPERTS, 2)),
            dma((chunks, 2, 4)), dma((chunks, 2, 4)),
            dma((chunks, 8)), dma((chunks, 8)),
            dma((chunks, 2, 4)), dma((chunks, 2, 4)),
            dma((chunks, 2)), dma((chunks, 2)),
            dma((EXPERTS, 2)), dma((EXPERTS, 2)),
            dma((EXPERTS,)), dma((EXPERTS,)),
        ],
        compiler_params=pltpu.CompilerParams(
            collective_id=0, has_side_effects=True, vmem_limit_bytes=60 * 1024 * 1024
        ),
    )(expert_ids.T, tokens, w_gate, w_up)


def solution(mesh):
    in_specs = (
        P("row", "layer"),
        P(),
        P(None, "layer", ("row", "col")),
        P(None, "layer", ("row", "col")),
    )
    out_specs = P(None, ("col", "layer"), "row")
    return jax.shard_map(shards, mesh=mesh, in_specs=in_specs, out_specs=out_specs, check_vma=False)
```

time: 270 us -> 93.5 us (0.35)
  waiting for transfers between devices: 152 us -> 0 us
  Pallas kernels: 0 us -> 91.7 us
  local copies, waits for them, and re-layouts: 80.4 us -> 1.72 us
  between operations: 15 us -> 0.01 us
  other arithmetic: 12.1 us -> 0 us
  matrix products: 9.66 us -> 0 us
    pallas_call x0 -> x1, Pallas kernels: none -> 91.7 us  [shards(): pl.pallas_call(kernel, name='experts', out_shape=jax.ShapeDtypeStruct((EX...]
    all_gather x2 -> x0, waiting for transfers between devices: 88.9 us -> none  [on_gathered_pieces(): done.append(jax.vmap(apply)(lax.all_gather(piece, axis), starts))]
    reduce_scatter x1 -> x0, waiting for transfers between devices: 62 us -> none  [shards(): parts = lax.psum_scatter(totals, 'layer', scatter_dimension=2, tiled=True)]
    unnamed x18 -> x1, local copies, waits for them, and re-layouts: 46.3 us -> 1.72 us
    all_gather x2 -> x0, local copies, waits for them, and re-layouts: 12.2 us -> none  [on_gathered_pieces(): done.append(jax.vmap(apply)(lax.all_gather(piece, axis), starts))]
    dot_general x2 -> x0, matrix products: 9.66 us -> none  [project(): jnp.einsum('ecd,pedf->pecf', slot_rows, piece, preferred_element_type=jnp...]
    reshape x1 -> x0, local copies, waits for them, and re-layouts: 6.73 us -> none  [laid_out(): tiles.reshape(*shape[:dim], shape[dim] * shape[dim + 1], *shape[dim + 2:])]
    transpose x1 -> x0, local copies, waits for them, and re-layouts: 6.3 us -> none  [laid_out(): tiles = jnp.moveaxis(tiles, 0, dim)]
  transfers between devices with their start and end apart: 4 -> 0, of which waited for: 3 -> 0; matrix products, arithmetic and copies ran while one was open for 26% -> 0% of each run, Pallas kernels for 0% -> 0%
where the time goes in v2:
time: 93.5 us; the launch traced here: 93.4 us
  Pallas kernels  91.7 us (98%)
  local copies, waits for them, and re-layouts  1.72 us (2%)
    pallas_call x1, Pallas kernels, shards(): pl.pallas_call(kernel, name='experts', out_shape=jax.ShapeDtypeStruct((EX...  91.7 us

profile of v2, /device:TPU:1, one launch (start us, length us, event | category | flops | bytes accessed | tf_op | source)
XLA Modules:
  0.0 93.4 jit_solution(14197706936541659005)
XLA Ops:
  0.0 91.7 %experts.1 = bf16[2,80,1024]{2,1,0:T(8,128)(2,1)} custom-call(s32[2,5120]{1,0:T(2,128)} %bitcast.1, bf16[640,1536]{1,0:T(8,128)(2,1)} %tok_ref.1, bf16[2,1536,128]{2,1,0:T(8,128)(2,1)} %wg_ref.1, bf16[2,1536,128]{2,1,0:T(8,128)(2,1)} %wu_ref.1), custom_call_target="tpu_custom_call" | custom-call | tf_op jit(solution)/shard_map/experts/pallas_call | solution.py:336
  91.7 1.7 %copy.6 = bf16[2,80,1024]{2,1,0:T(8,128)(2,1)} copy(bf16[2,80,1024]{2,1,0:T(8,128)(2,1)} %experts.1) | data formatting | bytes 655360

commit v3 on v2

v3 whole, which is shorter than its diff:
```python
import jax
import jax.numpy as jnp
from jax import lax
from jax.experimental import pallas as pl
from jax.experimental.pallas import tpu as pltpu
from jax.sharding import PartitionSpec as P

MESH = pl.DeviceIdType.MESH
ROWS = 8
BLOCK = 80
DEPTH = 1536
QUARTER = DEPTH // 4
HALF = DEPTH // 2
LANES = 128
EXPERTS = 2
CHUNKS = ((0, 0), (1, 0), (0, 1), (1, 1))
SIDEWAYS = (0, 1)
Y_STEP = (0, 1, 3, 2)
PIECES = ((0, 1), (1, 2), (3, 1))

PLAN = (
    "w11", "r001", "r111", "w01", "w00", "r011", "r002", "r112", "r101", "r012", "r003", "r113",
    "r102", "r013", "r004", "r114", "r103", "t0", "r311", "r301", "t1", "w10", "a012", "a002",
    "r211", "r201", "r312", "r302", "a102", "a003", "a013", "a112", "r212", "r202", "r303", "r313",
    "a014", "a103", "f00", "f01", "a113", "a004", "r203", "r314", "a015", "a104", "r213", "r204",
    "a114", "t3", "p010", "a105", "p011", "f11", "f10", "t2", "h01", "p0001", "a301", "a311",
    "h00", "p1101", "a201", "a211", "h11", "a302", "a312", "p0201", "h02", "a202", "a212", "a303",
    "a313", "a203", "a213", "p1201", "h12", "a304", "p100", "a214", "p101", "h10", "p320", "p3101",
    "p321", "p3001", "p220", "p2101", "p2001", "p221", "o0", "m0", "o1", "m1", "b0", "b1",
)


def ring_steps(odd):
    return (3, 4) if odd else (4, 3)


class Copy:
    def __init__(self, src, dst, send_sem, recv_sem, device):
        self.copy = pltpu.make_async_remote_copy(
            src_ref=src, dst_ref=dst, send_sem=send_sem, recv_sem=recv_sem,
            device_id=device, device_id_type=MESH,
        )
        self.copy.start()
        self.arrived = False

    def wait(self):
        if not self.arrived:
            self.copy.wait_recv()
        self.arrived = True


def kernel(
    ids_hbm, tok_hbm, wg_hbm, wu_hbm, out_ref,
    ids_ref, tok_ref, wbuf, placed, sums, slots, part, from_core, from_hi, sent, back,
    in_s, w_s, w_r, wf_s, wf_r, rs_s, rs_r, x_s, x_r, ag_s, ag_r, c_s, c_r, h_s, h_r, o_s, o_r,
):
    z = lax.axis_index("row")
    col = lax.axis_index("col")
    layer = lax.axis_index("layer")
    xl, y = col // 4, col % 4
    xh, core = layer // 2, layer % 2

    def at_row(step):
        return (lax.rem(z + step + ROWS, ROWS), col, layer)

    def at_y(step):
        return (z, xl * 4 + lax.rem(y + step, 4), layer)

    pair = (z, (1 - xl) * 4 + y, layer)
    other_core = (z, col, xh * 2 + (1 - core))
    other_hi = (z, col, (1 - xh) * 2 + core)

    barrier = pltpu.get_barrier_semaphore()
    partners = [at_row(1), at_row(-1), at_y(1), at_y(3), pair, other_core, other_hi]
    for partner in partners:
        pl.semaphore_signal(barrier, inc=1, device_id=partner, device_id_type=MESH)

    ids_in = pltpu.make_async_copy(ids_hbm, ids_ref, in_s.at[0])
    tok_in = pltpu.make_async_copy(tok_hbm, tok_ref, in_s.at[1])
    w_in = [
        [
            pltpu.make_async_copy(
                ref.at[e], wbuf.at[0, e, :, pl.ds(g * LANES, LANES)], in_s.at[2 + 2 * e + g]
            )
            for g, ref in enumerate((wg_hbm, wu_hbm))
        ]
        for e in range(EXPERTS)
    ]
    for copy in (ids_in, tok_in, *w_in[0], *w_in[1]):
        copy.start()

    copies = {}

    def send(key, src, dst, send_sem, recv_sem, device):
        copies[key] = Copy(src, dst, send_sem, recv_sem, device)

    def send_weights(e, i):
        for d in range(2):
            half = i if d == 0 else 1 - i
            rows = pl.ds(half * HALF, HALF)
            send(
                ("w", e, d, half), wbuf.at[0, e, rows, :], wbuf.at[2 - d, e, rows, :],
                w_s.at[e, d, half], w_r.at[e, d, half], at_y(1 if d == 0 else 3),
            )

    def pass_weights(e, d):
        copies["w", e, d, d].wait()
        rows = pl.ds(d * HALF, HALF)
        send(
            ("f", e, d), wbuf.at[2 - d, e, rows, :], wbuf.at[3, e, rows, :],
            wf_s.at[e, d], wf_r.at[e, d], at_y(1 if d == 0 else 3),
        )

    def weights_done(e, piece):
        if piece == 1:
            for d in range(2):
                for half in range(2):
                    copies["w", e, d, half].wait()
        elif piece == 2:
            for d in range(2):
                copies["f", e, d].wait()

    count = tok_ref.shape[0]
    start = pl.multiple_of(z * count, LANES)
    rank = []

    def find_ranks():
        above = lax.broadcasted_iota(jnp.int32, (count, count), 0)
        right = lax.broadcasted_iota(jnp.int32, (count, count), 1)
        before = (above < right).astype(jnp.float32).astype(jnp.bfloat16)
        token = lax.broadcasted_iota(jnp.int32, (1, ids_ref.shape[1]), 1)
        for e in range(EXPERTS):
            named = (ids_ref[0:1, :] == e) | (ids_ref[1:2, :] == e)
            ahead = jnp.sum((named & (token < start)).astype(jnp.float32), axis=1, keepdims=True)
            here = pl.ds(start, count)
            own = (ids_ref[0:1, here] == e) | (ids_ref[1:2, here] == e)
            ones = jnp.broadcast_to(own.astype(jnp.float32), (16, count)).astype(jnp.bfloat16)
            within = jnp.dot(ones, before, preferred_element_type=jnp.float32)[0:1]
            rank.append(jnp.where(own, (within + ahead).astype(jnp.int32), -1))

    def slot_start(c, r):
        to_hi = xh if CHUNKS[c][1] else 1 - xh
        to_core = core if r else 1 - core
        return (col * 4 + to_hi * 2 + to_core) * BLOCK

    def place_rows(c):
        index = lax.broadcasted_iota(jnp.int32, (BLOCK, count), 0)
        slot = jnp.concatenate([index + slot_start(c, 0), index + slot_start(c, 1)], axis=0)
        pick = (slot == rank[CHUNKS[c][0]]).astype(jnp.float32).astype(jnp.bfloat16)
        for f in range(2):
            placed[c, :, f * HALF : (f + 1) * HALF] = jnp.dot(
                pick, tok_ref[:, f * HALF : (f + 1) * HALF], preferred_element_type=jnp.float32
            ).astype(jnp.bfloat16)

    def owner_lanes(k):
        return pl.ds(pl.multiple_of((k % 4) * QUARTER, LANES), QUARTER)

    def owner_rows(c, k):
        return placed.at[c, pl.ds(pl.multiple_of((k // 4) * BLOCK, 16), BLOCK), owner_lanes(k)]

    def reduce_step(c, d, s):
        sign, steps = 1 - 2 * d, ring_steps(c % 2)[d]
        k = lax.rem(z + sign * (steps - s + 1) + ROWS, ROWS)
        if s == 1:
            src = owner_rows(c, k)
        else:
            copies["r", c, d, s - 1].wait()
            src = sums.at[c, d, s - 2]
            src[...] = src[...] + owner_rows(c, k)[...]
        send(
            ("r", c, d, s), src, sums.at[c, d, s - 1],
            rs_s.at[c, d, s - 1], rs_r.at[c, d, s - 1], at_row(sign),
        )

    def slot_rows(c, k, side):
        first = pl.multiple_of((k // 4) * (2 * BLOCK) + side * BLOCK, 16)
        return slots.at[c, pl.ds(first, BLOCK), owner_lanes(k)]

    def both_sides(c, k):
        first = pl.multiple_of((k // 4) * (2 * BLOCK), 16)
        return slots.at[c, pl.ds(first, 2 * BLOCK), owner_lanes(k)]

    def to_pair(c, i, k):
        rows = slot_rows(c, k, xl)
        send(("x", c, i), rows, rows, x_s.at[c, i], x_r.at[c, i], pair)

    def finish_reduce(c):
        up, down = ring_steps(c % 2)
        copies["r", c, 0, up].wait()
        copies["r", c, 1, down].wait()
        mine = slot_rows(c, z, xl)
        mine[...] = sums[c, 0, up - 1] + sums[c, 1, down - 1] + owner_rows(c, z)[...]
        if c in SIDEWAYS:
            for d in range(2):
                gather_send(c, d, 1)
        to_pair(c, 0, z)

    def gather_send(c, d, s):
        sign = 1 - 2 * d
        k = lax.rem(z - sign * (s - 1) + ROWS, ROWS)
        rows = slot_rows(c, k, xl) if c in SIDEWAYS else both_sides(c, k)
        send(
            ("a", c, d, s), rows, rows, ag_s.at[c, d, s - 1], ag_r.at[c, d, s - 1], at_row(sign)
        )

    def gather_step(c, d, s):
        sign, steps = 1 - 2 * d, ring_steps(1 - c % 2)
        if s == 1:
            copies["x", c, 0].wait()
        else:
            copies["a", c, d, s - 1].wait()
        if s <= steps[d]:
            gather_send(c, d, s)
        if c in SIDEWAYS:
            to_pair(c, 1 + d * steps[0] + s - 2, lax.rem(z - sign * (s - 1) + ROWS, ROWS))

    def slots_done(c):
        for d in range(2):
            copies["a", c, d, ring_steps(1 - c % 2)[d]].wait()
        for i in range(8 if c in SIDEWAYS else 1):
            copies["x", c, i].wait()

    def project(c, piece, *rows):
        e = CHUNKS[c][0]
        first, number = PIECES[piece]
        slots_done(c)
        weights_done(e, piece)
        top, span = rows[0] * 2 * BLOCK, len(rows) * 2 * BLOCK
        for b in range(first, first + number):
            total = jnp.dot(
                slots[c, top : top + span, :], wbuf[b, e], preferred_element_type=jnp.float32
            )
            for i, row in enumerate(rows):
                for side in range(2):
                    at = (i * 2 + side) * BLOCK
                    part[c, row, b, side] = total[at : at + BLOCK]
        if 0 in rows:
            here = pl.ds(first, number)
            send(
                ("c", c, piece), part.at[c, 0, here], from_core.at[c, here],
                c_s.at[c, piece], c_r.at[c, piece], other_core,
            )

    def to_hi(c, piece):
        e = CHUNKS[c][0]
        first, number = PIECES[piece]
        copies["c", c, piece].wait()

        for b in range(first, first + number):
            for side in range(2):
                part[c, 1, b, side] = part[c, 1, b, side] + from_core[c, b, side]

        here = pl.ds(first, number)
        send(
            ("h", e, piece), part.at[c, 1, here], from_hi.at[e, here],
            h_s.at[e, piece], h_r.at[e, piece], other_hi,
        )

    def hidden(e, side, b):
        c = CHUNKS.index((e, 1))
        total = part[c, 1, b, side] + from_core[c, b, side] + from_hi[e, b, side]
        gate, up = total[:, :LANES], total[:, LANES:]
        return (gate / (1.0 + jnp.exp(-gate)) * up).astype(jnp.bfloat16)

    def finish_out(e):
        c = CHUNKS.index((e, 1))
        for piece in range(len(PIECES)):
            copies["h", e, piece].wait()
            copies["c", c, piece].wait()
        for b in range(4):
            sent[e, :, b * LANES : (b + 1) * LANES] = hidden(e, 1 - xl, b)
        send(("o", e), sent.at[e], back.at[e], o_s.at[e], o_r.at[e], pair)

    def finish_own(e):
        for b in range(4):
            out_ref[e, :, out_lanes(xl, b)] = hidden(e, xl, b)

    def out_lanes(side, b):
        return pl.ds(pl.multiple_of((side * 4 + lax.rem(y + Y_STEP[b], 4)) * LANES, LANES), LANES)

    def take_back(e):
        copies["o", e].wait()
        for b in range(4):
            out_ref[e, :, out_lanes(1 - xl, b)] = back[e, :, b * LANES : (b + 1) * LANES]

    ids_in.wait()
    find_ranks()
    tok_in.wait()
    for c in range(len(CHUNKS)):
        place_rows(c)
    for e in range(EXPERTS):
        for copy in w_in[e]:
            copy.wait()
    pl.semaphore_wait(barrier, len(partners))
    acts = {
        "w": send_weights, "f": pass_weights, "r": reduce_step, "t": finish_reduce, "a": gather_step,
        "p": project, "h": to_hi, "o": finish_out, "m": finish_own, "b": take_back,
    }
    for step in PLAN:
        acts[step[0]](*map(int, step[1:]))
    for copy in copies.values():
        copy.copy.wait_send()


def shards(tokens, expert_ids, w_gate, w_up):
    bf16, f32 = jnp.bfloat16, jnp.float32
    vmem, dma = pltpu.VMEM, pltpu.SemaphoreType.DMA
    chunks = len(CHUNKS)
    return pl.pallas_call(
        kernel,
        name="experts",
        out_shape=jax.ShapeDtypeStruct((EXPERTS, BLOCK, 1024), bf16),
        in_specs=[pl.BlockSpec(memory_space=pl.ANY)] * 4,
        out_specs=pl.BlockSpec(memory_space=pltpu.VMEM),
        scratch_shapes=[
            vmem(expert_ids.shape[::-1], jnp.int32),
            vmem(tokens.shape, bf16),
            vmem((4, EXPERTS, DEPTH, 2 * LANES), bf16),
            vmem((chunks, 2 * BLOCK, DEPTH), bf16),
            vmem((chunks, 2, 4, BLOCK, QUARTER), bf16),
            vmem((chunks, 4 * BLOCK, DEPTH), bf16),
            vmem((chunks, 2, 4, 2, BLOCK, 2 * LANES), f32),
            vmem((chunks, 4, 2, BLOCK, 2 * LANES), f32),
            vmem((EXPERTS, 4, 2, BLOCK, 2 * LANES), f32),
            vmem((EXPERTS, BLOCK, 4 * LANES), bf16),
            vmem((EXPERTS, BLOCK, 4 * LANES), bf16),
            dma((6,)),
            dma((EXPERTS, 2, 2)), dma((EXPERTS, 2, 2)),
            dma((EXPERTS, 2)), dma((EXPERTS, 2)),
            dma((chunks, 2, 4)), dma((chunks, 2, 4)),
            dma((chunks, 8)), dma((chunks, 8)),
            dma((chunks, 2, 4)), dma((chunks, 2, 4)),
            dma((chunks, 3)), dma((chunks, 3)),
            dma((EXPERTS, 3)), dma((EXPERTS, 3)),
            dma((EXPERTS,)), dma((EXPERTS,)),
        ],
        compiler_params=pltpu.CompilerParams(
            collective_id=0, has_side_effects=True, vmem_limit_bytes=60 * 1024 * 1024
        ),
    )(expert_ids.T, tokens, w_gate, w_up)


def solution(mesh):
    in_specs = (
        P("row", "layer"),
        P(),
        P(None, "layer", ("row", "col")),
        P(None, "layer", ("row", "col")),
    )
    out_specs = P(None, ("col", "layer"), "row")
    return jax.shard_map(shards, mesh=mesh, in_specs=in_specs, out_specs=out_specs, check_vma=False)
```

time: 93.5 us -> 87 us (0.930)
  the two profiles are of different devices: /device:TPU:1 before, /device:TPU:18 now
where the time goes in v3:
time: 87 us; the launch traced here: 86.9 us
  Pallas kernels  85.2 us (98%)
  local copies, waits for them, and re-layouts  1.72 us (2%)
    pallas_call x1, Pallas kernels, shards(): pl.pallas_call(kernel, name='experts', out_shape=jax.ShapeDtypeStruct((EX...  85.2 us

profile of v3, /device:TPU:18, one launch (start us, length us, event | category | flops | bytes accessed | tf_op | source)
XLA Modules:
  0.0 86.9 jit_solution(18171462082266098394)
XLA Ops:
  0.0 85.2 %experts.1 = bf16[2,80,1024]{2,1,0:T(8,128)(2,1)} custom-call(s32[2,5120]{1,0:T(2,128)} %bitcast.1, bf16[640,1536]{1,0:T(8,128)(2,1)} %tok_hbm.1, bf16[2,1536,128]{2,1,0:T(8,128)(2,1)} %wg_hbm.1, bf16[2,1536,128]{2,1,0:T(8,128)(2,1)} %wu_hbm.1), custom_call_target="tpu_custom_call" | custom-call | tf_op jit(solution)/shard_map/experts/pallas_call | solution.py:309
  85.2 1.7 %copy.6 = bf16[2,80,1024]{2,1,0:T(8,128)(2,1)} copy(bf16[2,80,1024]{2,1,0:T(8,128)(2,1)} %experts.1) | data formatting | bytes 655360

commit v4 on v3

--- a/solution.py
+++ b/solution.py
@@ -14,19 +14,22 @@
 LANES = 128
 EXPERTS = 2
 CHUNKS = ((0, 0), (1, 0), (0, 1), (1, 1))
-SIDEWAYS = (0, 1)
+TREES = (0,)
+SPREADS = ()
+SIDEWAYS = (0,)
 Y_STEP = (0, 1, 3, 2)
 PIECES = ((0, 1), (1, 2), (3, 1))
 
 PLAN = (
-    "w11", "r001", "r111", "w01", "w00", "r011", "r002", "r112", "r101", "r012", "r003", "r113",
-    "r102", "r013", "r004", "r114", "r103", "t0", "r311", "r301", "t1", "w10", "a012", "a002",
-    "r211", "r201", "r312", "r302", "a102", "a003", "a013", "a112", "r212", "r202", "r303", "r313",
-    "a014", "a103", "f00", "f01", "a113", "a004", "r203", "r314", "a015", "a104", "r213", "r204",
-    "a114", "t3", "p010", "a105", "p011", "f11", "f10", "t2", "h01", "p0001", "a301", "a311",
-    "h00", "p1101", "a201", "a211", "h11", "a302", "a312", "p0201", "h02", "a202", "a212", "a303",
-    "a313", "a203", "a213", "p1201", "h12", "a304", "p100", "a214", "p101", "h10", "p320", "p3101",
-    "p321", "p3001", "p220", "p2101", "p2001", "p221", "o0", "m0", "o1", "m1", "b0", "b1",
+    "r001", "r111", "r311", "r301", "w11", "w00", "w01", "r011", "r112", "r312", "r101", "r012",
+    "r002", "r201", "r113", "r313", "r102", "r302", "t0", "r211", "r202", "r114", "r103", "r303",
+    "a012", "a002", "r212", "f00", "f01", "r203", "t1", "a013", "r314", "r213", "a003", "a101",
+    "r204", "a014", "t3", "a004", "a111", "a015", "w10", "a311", "a102", "a301", "t2", "p000",
+    "a112", "p010", "p001", "p011", "h00", "a211", "a103", "a312", "h01", "p0201", "a302", "a113",
+    "h02", "a104", "a212", "a201", "a303", "a313", "f11", "f10", "p1001", "p1101", "h10", "a202",
+    "a213", "h11", "a304", "a203", "a214", "p120", "p300", "p3101", "p121", "h12", "p3201", "p301",
+    "p2101", "p2001", "p2201", "o10", "m10", "o01", "m01", "o00", "o11", "o02", "m11", "m02",
+    "m00", "b10", "o12", "m12", "b01", "b00", "b11", "b02", "b12",
 )
 
 
@@ -71,7 +74,8 @@
     other_hi = (z, col, (1 - xh) * 2 + core)
 
     barrier = pltpu.get_barrier_semaphore()
-    partners = [at_row(1), at_row(-1), at_y(1), at_y(3), pair, other_core, other_hi]
+    rows_met = (1, -1, 2, -2) if TREES or SPREADS else (1, -1)
+    partners = [*map(at_row, rows_met), at_y(1), at_y(3), pair, other_core, other_hi]
     for partner in partners:
         pl.semaphore_signal(barrier, inc=1, device_id=partner, device_id_type=MESH)
 
@@ -158,19 +162,38 @@
     def owner_rows(c, k):
         return placed.at[c, pl.ds(pl.multiple_of((k // 4) * BLOCK, 16), BLOCK), owner_lanes(k)]
 
+    def reduce_send(c, d, s, src, hops):
+        send(
+            ("r", c, d, s), src, sums.at[c, d, s - 1],
+            rs_s.at[c, d, s - 1], rs_r.at[c, d, s - 1], at_row((1 - 2 * d) * hops),
+        )
+
     def reduce_step(c, d, s):
         sign, steps = 1 - 2 * d, ring_steps(c % 2)[d]
-        k = lax.rem(z + sign * (steps - s + 1) + ROWS, ROWS)
-        if s == 1:
-            src = owner_rows(c, k)
+
+        def rows_for(distance):
+            return owner_rows(c, lax.rem(z + sign * distance + ROWS, ROWS))
+
+        if c not in TREES:
+            src = rows_for(steps - s + 1)
+            if s > 1:
+                copies["r", c, d, s - 1].wait()
+                sums[c, d, s - 2] = sums[c, d, s - 2] + src[...]
+                src = sums.at[c, d, s - 2]
+            reduce_send(c, d, s, src, 1)
+        elif s == 1:
+            reduce_send(c, d, 1, rows_for(3), 1)
+            if steps == 4:
+                reduce_send(c, d, 2, rows_for(4), 2)
+            reduce_send(c, d, 4, rows_for(1), 1)
         else:
-            copies["r", c, d, s - 1].wait()
-            src = sums.at[c, d, s - 2]
-            src[...] = src[...] + owner_rows(c, k)[...]
-        send(
-            ("r", c, d, s), src, sums.at[c, d, s - 1],
-            rs_s.at[c, d, s - 1], rs_r.at[c, d, s - 1], at_row(sign),
-        )
+            copies["r", c, d, 1].wait()
+            total = sums[c, d, 0] + rows_for(2)[...]
+            if steps == 4:
+                copies["r", c, d, 2].wait()
+                total = total + sums[c, d, 1]
+            sums[c, d, 0] = total
+            reduce_send(c, d, 3, sums.at[c, d, 0], 2)
 
     def slot_rows(c, k, side):
         first = pl.multiple_of((k // 4) * (2 * BLOCK) + side * BLOCK, 16)
@@ -185,38 +208,55 @@
         send(("x", c, i), rows, rows, x_s.at[c, i], x_r.at[c, i], pair)
 
     def finish_reduce(c):
-        up, down = ring_steps(c % 2)
-        copies["r", c, 0, up].wait()
-        copies["r", c, 1, down].wait()
+        total = owner_rows(c, z)[...]
+        for d in range(2):
+            for s in (3, 4) if c in TREES else (ring_steps(c % 2)[d],):
+                copies["r", c, d, s].wait()
+                total = total + sums[c, d, s - 1]
         mine = slot_rows(c, z, xl)
-        mine[...] = sums[c, 0, up - 1] + sums[c, 1, down - 1] + owner_rows(c, z)[...]
+        mine[...] = total
         if c in SIDEWAYS:
             for d in range(2):
                 gather_send(c, d, 1)
         to_pair(c, 0, z)
 
+    def gather_block(c, d, distance):
+        return lax.rem(z - (1 - 2 * d) * distance + ROWS, ROWS)
+
+    def gather_copy(c, d, s, distance, hops):
+        k = gather_block(c, d, distance)
+        rows = slot_rows(c, k, xl) if c in SIDEWAYS else both_sides(c, k)
+        send(
+            ("a", c, d, s), rows, rows, ag_s.at[c, d, s - 1], ag_r.at[c, d, s - 1],
+            at_row((1 - 2 * d) * hops),
+        )
+
     def gather_send(c, d, s):
-        sign = 1 - 2 * d
-        k = lax.rem(z - sign * (s - 1) + ROWS, ROWS)
-        rows = slot_rows(c, k, xl) if c in SIDEWAYS else both_sides(c, k)
-        send(
-            ("a", c, d, s), rows, rows, ag_s.at[c, d, s - 1], ag_r.at[c, d, s - 1], at_row(sign)
-        )
+        steps = ring_steps(1 - c % 2)[d]
+        if c not in SPREADS:
+            if s <= steps:
+                gather_copy(c, d, s, s - 1, 1)
+        elif s == 1:
+            gather_copy(c, d, 1, 0, 1)
+            gather_copy(c, d, 2, 0, 2)
+        elif s == 3:
+            gather_copy(c, d, 3, 2, 1)
+            if steps == 4:
+                gather_copy(c, d, 4, 2, 2)
 
     def gather_step(c, d, s):
-        sign, steps = 1 - 2 * d, ring_steps(1 - c % 2)
         if s == 1:
             copies["x", c, 0].wait()
         else:
             copies["a", c, d, s - 1].wait()
-        if s <= steps[d]:
-            gather_send(c, d, s)
+        gather_send(c, d, s)
         if c in SIDEWAYS:
-            to_pair(c, 1 + d * steps[0] + s - 2, lax.rem(z - sign * (s - 1) + ROWS, ROWS))
+            to_pair(c, 1 + d * ring_steps(1 - c % 2)[0] + s - 2, gather_block(c, d, s - 1))
 
     def slots_done(c):
         for d in range(2):
-            copies["a", c, d, ring_steps(1 - c % 2)[d]].wait()
+            for s in range(ring_steps(1 - c % 2)[d]):
+                copies["a", c, d, s + 1].wait()
         for i in range(8 if c in SIDEWAYS else 1):
             copies["x", c, i].wait()
 
@@ -262,25 +302,31 @@
         gate, up = total[:, :LANES], total[:, LANES:]
         return (gate / (1.0 + jnp.exp(-gate)) * up).astype(jnp.bfloat16)
 
-    def finish_out(e):
-        c = CHUNKS.index((e, 1))
-        for piece in range(len(PIECES)):
-            copies["h", e, piece].wait()
-            copies["c", c, piece].wait()
-        for b in range(4):
+    def positions(piece):
+        first, number = PIECES[piece]
+        return range(first, first + number), pl.ds(first * LANES, number * LANES)
+
+    def finish_out(e, piece):
+        copies["h", e, piece].wait()
+        copies["c", CHUNKS.index((e, 1)), piece].wait()
+        blocks, lanes = positions(piece)
+        for b in blocks:
             sent[e, :, b * LANES : (b + 1) * LANES] = hidden(e, 1 - xl, b)
-        send(("o", e), sent.at[e], back.at[e], o_s.at[e], o_r.at[e], pair)
-
-    def finish_own(e):
-        for b in range(4):
+        send(
+            ("o", e, piece), sent.at[e, :, lanes], back.at[e, :, lanes],
+            o_s.at[e, piece], o_r.at[e, piece], pair,
+        )
+
+    def finish_own(e, piece):
+        for b in positions(piece)[0]:
             out_ref[e, :, out_lanes(xl, b)] = hidden(e, xl, b)
 
     def out_lanes(side, b):
         return pl.ds(pl.multiple_of((side * 4 + lax.rem(y + Y_STEP[b], 4)) * LANES, LANES), LANES)
 
-    def take_back(e):
-        copies["o", e].wait()
-        for b in range(4):
+    def take_back(e, piece):
+        copies["o", e, piece].wait()
+        for b in positions(piece)[0]:
             out_ref[e, :, out_lanes(1 - xl, b)] = back[e, :, b * LANES : (b + 1) * LANES]
 
     ids_in.wait()
@@ -332,7 +378,7 @@
             dma((chunks, 2, 4)), dma((chunks, 2, 4)),
             dma((chunks, 3)), dma((chunks, 3)),
             dma((EXPERTS, 3)), dma((EXPERTS, 3)),
-            dma((EXPERTS,)), dma((EXPERTS,)),
+            dma((EXPERTS, 3)), dma((EXPERTS, 3)),
         ],
         compiler_params=pltpu.CompilerParams(
             collective_id=0, has_side_effects=True, vmem_limit_bytes=60 * 1024 * 1024

time: 87 us -> 82 us (0.943)
  the two profiles are of different devices: /device:TPU:18 before, /device:TPU:1 now
where the time goes in v4:
time: 82 us; the launch traced here: 81.9 us
  Pallas kernels  80.2 us (98%)
  local copies, waits for them, and re-layouts  1.72 us (2%)
    pallas_call x1, Pallas kernels, shards(): pl.pallas_call(kernel, name='experts', out_shape=jax.ShapeDtypeStruct((EX...  80.2 us
    unnamed x1, local copies, waits for them, and re-layouts  1.72 us

profile of v4, /device:TPU:1, one launch (start us, length us, event | category | flops | bytes accessed | tf_op | source)
XLA Modules:
  0.0 81.9 jit_solution(17417638842942261183)
XLA Ops:
  0.0 80.2 %experts.1 = bf16[2,80,1024]{2,1,0:T(8,128)(2,1)} custom-call(s32[2,5120]{1,0:T(2,128)} %bitcast.1, bf16[640,1536]{1,0:T(8,128)(2,1)} %tok_hbm.1, bf16[2,1536,128]{2,1,0:T(8,128)(2,1)} %wg_hbm.1, bf16[2,1536,128]{2,1,0:T(8,128)(2,1)} %wu_hbm.1), custom_call_target="tpu_custom_call" | custom-call | tf_op jit(solution)/shard_map/experts/pallas_call | solution.py:355
  80.2 1.7 %copy.6 = bf16[2,80,1024]{2,1,0:T(8,128)(2,1)} copy(bf16[2,80,1024]{2,1,0:T(8,128)(2,1)} %experts.1) | data formatting | bytes 655360

commit v5 on v4

--- a/solution.py
+++ b/solution.py
@@ -14,22 +14,23 @@
 LANES = 128
 EXPERTS = 2
 CHUNKS = ((0, 0), (1, 0), (0, 1), (1, 1))
-TREES = (0,)
+TREES = ()
 SPREADS = ()
 SIDEWAYS = (0,)
 Y_STEP = (0, 1, 3, 2)
 PIECES = ((0, 1), (1, 2), (3, 1))
 
 PLAN = (
-    "r001", "r111", "r311", "r301", "w11", "w00", "w01", "r011", "r112", "r312", "r101", "r012",
-    "r002", "r201", "r113", "r313", "r102", "r302", "t0", "r211", "r202", "r114", "r103", "r303",
-    "a012", "a002", "r212", "f00", "f01", "r203", "t1", "a013", "r314", "r213", "a003", "a101",
-    "r204", "a014", "t3", "a004", "a111", "a015", "w10", "a311", "a102", "a301", "t2", "p000",
-    "a112", "p010", "p001", "p011", "h00", "a211", "a103", "a312", "h01", "p0201", "a302", "a113",
-    "h02", "a104", "a212", "a201", "a303", "a313", "f11", "f10", "p1001", "p1101", "h10", "a202",
-    "a213", "h11", "a304", "a203", "a214", "p120", "p300", "p3101", "p121", "h12", "p3201", "p301",
-    "p2101", "p2001", "p2201", "o10", "m10", "o01", "m01", "o00", "o11", "o02", "m11", "m02",
-    "m00", "b10", "o12", "m12", "b01", "b00", "b11", "b02", "b12",
+    "w00", "r001", "r211", "r111", "r301", "w01", "r011", "r002", "r212", "r101", "r112", "r302",
+    "r012", "r003", "r311", "w10", "r102", "r113", "r201", "r013", "f01", "r004", "f00", "r312",
+    "r103", "r114", "r202", "t0", "r313", "r303", "t1", "r203", "w11", "a012", "a002", "r314",
+    "a101", "r213", "r204", "a013", "a111", "t3", "a003", "a102", "a014", "t2", "a311", "a301",
+    "f10", "f11", "a004", "a112", "a015", "q000", "q010", "a103", "a211", "a201", "k000", "k010",
+    "a312", "a302", "q001", "q011", "k001", "a113", "k011", "a104", "q020", "q021", "k020", "k021",
+    "a212", "a202", "a313", "a303", "p1001", "p1101", "h10", "a213", "a203", "h11", "a304", "a214",
+    "p1201", "p310", "p3001", "p311", "p3201", "h12", "p2101", "p200", "p2201", "p201", "o10", "m10",
+    "o01", "m01", "o11", "o00", "m00", "m11", "o02", "m02", "b10", "o12", "m12", "b01",
+    "b11", "b00", "b02", "b12",
 )
 
 
@@ -53,8 +54,8 @@
 
 
 def kernel(
-    ids_hbm, tok_hbm, wg_hbm, wu_hbm, out_ref,
-    ids_ref, tok_ref, wbuf, placed, sums, slots, part, from_core, from_hi, sent, back,
+    ids_ref, tok_hbm, wg_hbm, wu_hbm, out_ref,
+    tok_ref, wbuf, placed, sums, slots, part, from_core, from_hi, sent, back,
     in_s, w_s, w_r, wf_s, wf_r, rs_s, rs_r, x_s, x_r, ag_s, ag_r, c_s, c_r, h_s, h_r, o_s, o_r,
 ):
     z = lax.axis_index("row")
@@ -79,19 +80,25 @@
     for partner in partners:
         pl.semaphore_signal(barrier, inc=1, device_id=partner, device_id_type=MESH)
 
-    ids_in = pltpu.make_async_copy(ids_hbm, ids_ref, in_s.at[0])
-    tok_in = pltpu.make_async_copy(tok_hbm, tok_ref, in_s.at[1])
+    tok_in = pltpu.make_async_copy(tok_hbm, tok_ref, in_s.at[0])
     w_in = [
         [
             pltpu.make_async_copy(
-                ref.at[e], wbuf.at[0, e, :, pl.ds(g * LANES, LANES)], in_s.at[2 + 2 * e + g]
+                ref.at[e], wbuf.at[0, e, :, pl.ds(g * LANES, LANES)], in_s.at[1 + 2 * e + g]
             )
             for g, ref in enumerate((wg_hbm, wu_hbm))
         ]
         for e in range(EXPERTS)
     ]
-    for copy in (ids_in, tok_in, *w_in[0], *w_in[1]):
+    for copy in (*w_in[1], tok_in, *w_in[0]):
         copy.start()
+    here = set()
+
+    def once(*what):
+        if what in here:
+            return False
+        here.add(what)
+        return True
 
     copies = {}
 
@@ -99,6 +106,9 @@
         copies[key] = Copy(src, dst, send_sem, recv_sem, device)
 
     def send_weights(e, i):
+        if once("w", e):
+            for copy in w_in[e]:
+                copy.wait()
         for d in range(2):
             half = i if d == 0 else 1 - i
             rows = pl.ds(half * HALF, HALF)
@@ -136,8 +146,8 @@
         for e in range(EXPERTS):
             named = (ids_ref[0:1, :] == e) | (ids_ref[1:2, :] == e)
             ahead = jnp.sum((named & (token < start)).astype(jnp.float32), axis=1, keepdims=True)
-            here = pl.ds(start, count)
-            own = (ids_ref[0:1, here] == e) | (ids_ref[1:2, here] == e)
+            lanes = pl.ds(start, count)
+            own = (ids_ref[0:1, lanes] == e) | (ids_ref[1:2, lanes] == e)
             ones = jnp.broadcast_to(own.astype(jnp.float32), (16, count)).astype(jnp.bfloat16)
             within = jnp.dot(ones, before, preferred_element_type=jnp.float32)[0:1]
             rank.append(jnp.where(own, (within + ahead).astype(jnp.int32), -1))
@@ -148,6 +158,9 @@
         return (col * 4 + to_hi * 2 + to_core) * BLOCK
 
     def place_rows(c):
+        if once("ids"):
+            find_ranks()
+            tok_in.wait()
         index = lax.broadcasted_iota(jnp.int32, (BLOCK, count), 0)
         slot = jnp.concatenate([index + slot_start(c, 0), index + slot_start(c, 1)], axis=0)
         pick = (slot == rank[CHUNKS[c][0]]).astype(jnp.float32).astype(jnp.bfloat16)
@@ -170,6 +183,8 @@
 
     def reduce_step(c, d, s):
         sign, steps = 1 - 2 * d, ring_steps(c % 2)[d]
+        if once("p", c):
+            place_rows(c)
 
         def rows_for(distance):
             return owner_rows(c, lax.rem(z + sign * distance + ROWS, ROWS))
@@ -253,12 +268,46 @@
         if c in SIDEWAYS:
             to_pair(c, 1 + d * ring_steps(1 - c % 2)[0] + s - 2, gather_block(c, d, s - 1))
 
-    def slots_done(c):
+    def slots_done(c, own_only=False):
         for d in range(2):
             for s in range(ring_steps(1 - c % 2)[d]):
                 copies["a", c, d, s + 1].wait()
-        for i in range(8 if c in SIDEWAYS else 1):
-            copies["x", c, i].wait()
+        if not own_only:
+            for i in range(8 if c in SIDEWAYS else 1):
+                copies["x", c, i].wait()
+
+    def project_side(c, piece, s):
+        e = CHUNKS[c][0]
+        first, number = PIECES[piece]
+        side = xl if s == 0 else 1 - xl
+        slots_done(c, s == 0)
+        weights_done(e, piece)
+        low = pl.multiple_of(side * BLOCK, 16)
+        rows = jnp.concatenate(
+            [slots[c, pl.ds(low, BLOCK), :], slots[c, pl.ds(low + 2 * BLOCK, BLOCK), :]], axis=0
+        )
+        for b in range(first, first + number):
+            total = jnp.dot(rows, wbuf[b, e], preferred_element_type=jnp.float32)
+            for r in range(2):
+                part[c, r, b, side] = total[r * BLOCK : (r + 1) * BLOCK]
+        span = pl.ds(first, number)
+        send(
+            ("c", c, piece, s), part.at[c, 0, span, side], from_core.at[c, span, side],
+            c_s.at[c, piece, s], c_r.at[c, piece, s], other_core,
+        )
+
+    def to_hi_side(c, piece, s):
+        e = CHUNKS[c][0]
+        first, number = PIECES[piece]
+        side = xl if s == 0 else 1 - xl
+        copies["c", c, piece, s].wait()
+        for b in range(first, first + number):
+            part[c, 1, b, side] = part[c, 1, b, side] + from_core[c, b, side]
+        span = pl.ds(first, number)
+        send(
+            ("h", e, piece, s), part.at[c, 1, span, side], from_hi.at[e, span, side],
+            h_s.at[e, piece, s], h_r.at[e, piece, s], other_hi,
+        )
 
     def project(c, piece, *rows):
         e = CHUNKS[c][0]
@@ -275,25 +324,25 @@
                     at = (i * 2 + side) * BLOCK
                     part[c, row, b, side] = total[at : at + BLOCK]
         if 0 in rows:
-            here = pl.ds(first, number)
+            span = pl.ds(first, number)
             send(
-                ("c", c, piece), part.at[c, 0, here], from_core.at[c, here],
-                c_s.at[c, piece], c_r.at[c, piece], other_core,
+                ("c", c, piece, 0), part.at[c, 0, span], from_core.at[c, span],
+                c_s.at[c, piece, 0], c_r.at[c, piece, 0], other_core,
             )
 
     def to_hi(c, piece):
         e = CHUNKS[c][0]
         first, number = PIECES[piece]
-        copies["c", c, piece].wait()
+        copies["c", c, piece, 0].wait()
 
         for b in range(first, first + number):
             for side in range(2):
                 part[c, 1, b, side] = part[c, 1, b, side] + from_core[c, b, side]
 
-        here = pl.ds(first, number)
-        send(
-            ("h", e, piece), part.at[c, 1, here], from_hi.at[e, here],
-            h_s.at[e, piece], h_r.at[e, piece], other_hi,
+        span = pl.ds(first, number)
+        send(
+            ("h", e, piece, 0), part.at[c, 1, span], from_hi.at[e, span],
+            h_s.at[e, piece, 0], h_r.at[e, piece, 0], other_hi,
         )
 
     def hidden(e, side, b):
@@ -307,8 +356,9 @@
         return range(first, first + number), pl.ds(first * LANES, number * LANES)
 
     def finish_out(e, piece):
-        copies["h", e, piece].wait()
-        copies["c", CHUNKS.index((e, 1)), piece].wait()
+        for s in range(2 if CHUNKS.index((e, 0)) in SIDEWAYS else 1):
+            copies["h", e, piece, s].wait()
+        copies["c", CHUNKS.index((e, 1)), piece, 0].wait()
         blocks, lanes = positions(piece)
         for b in blocks:
             sent[e, :, b * LANES : (b + 1) * LANES] = hidden(e, 1 - xl, b)
@@ -329,18 +379,10 @@
         for b in positions(piece)[0]:
             out_ref[e, :, out_lanes(1 - xl, b)] = back[e, :, b * LANES : (b + 1) * LANES]
 
-    ids_in.wait()
-    find_ranks()
-    tok_in.wait()
-    for c in range(len(CHUNKS)):
-        place_rows(c)
-    for e in range(EXPERTS):
-        for copy in w_in[e]:
-            copy.wait()
     pl.semaphore_wait(barrier, len(partners))
     acts = {
         "w": send_weights, "f": pass_weights, "r": reduce_step, "t": finish_reduce, "a": gather_step,
-        "p": project, "h": to_hi, "o": finish_out, "m": finish_own, "b": take_back,
+        "p": project, "h": to_hi, "q": project_side, "k": to_hi_side, "o": finish_out, "m": finish_own, "b": take_back,
     }
     for step in PLAN:
         acts[step[0]](*map(int, step[1:]))
@@ -356,10 +398,9 @@
         kernel,
         name="experts",
         out_shape=jax.ShapeDtypeStruct((EXPERTS, BLOCK, 1024), bf16),
-        in_specs=[pl.BlockSpec(memory_space=pl.ANY)] * 4,
+        in_specs=[pl.BlockSpec(memory_space=pltpu.VMEM)] + [pl.BlockSpec(memory_space=pl.ANY)] * 3,
         out_specs=pl.BlockSpec(memory_space=pltpu.VMEM),
         scratch_shapes=[
-            vmem(expert_ids.shape[::-1], jnp.int32),
             vmem(tokens.shape, bf16),
             vmem((4, EXPERTS, DEPTH, 2 * LANES), bf16),
             vmem((chunks, 2 * BLOCK, DEPTH), bf16),
@@ -370,18 +411,18 @@
             vmem((EXPERTS, 4, 2, BLOCK, 2 * LANES), f32),
             vmem((EXPERTS, BLOCK, 4 * LANES), bf16),
             vmem((EXPERTS, BLOCK, 4 * LANES), bf16),
-            dma((6,)),
+            dma((5,)),
             dma((EXPERTS, 2, 2)), dma((EXPERTS, 2, 2)),
             dma((EXPERTS, 2)), dma((EXPERTS, 2)),
             dma((chunks, 2, 4)), dma((chunks, 2, 4)),
             dma((chunks, 8)), dma((chunks, 8)),
             dma((chunks, 2, 4)), dma((chunks, 2, 4)),
-            dma((chunks, 3)), dma((chunks, 3)),
-            dma((EXPERTS, 3)), dma((EXPERTS, 3)),
+            dma((chunks, 3, 2)), dma((chunks, 3, 2)),
+            dma((EXPERTS, 3, 2)), dma((EXPERTS, 3, 2)),
             dma((EXPERTS, 3)), dma((EXPERTS, 3)),
         ],
         compiler_params=pltpu.CompilerParams(
-            collective_id=0, has_side_effects=True, vmem_limit_bytes=60 * 1024 * 1024
+            collective_id=0, has_side_effects=True, vmem_limit_bytes=55920000
         ),
     )(expert_ids.T, tokens, w_gate, w_up)
 

time: 82 us -> 80.5 us (0.982)
  Pallas kernels: 80.2 us -> 78.9 us
    pallas_call x1, Pallas kernels: 80.2 us -> 78.9 us  [shards(): pl.pallas_call(kernel, name='experts', out_shape=jax.ShapeDtypeStruct((EX...]
    unnamed x1 -> x3, local copies, waits for them, and re-layouts: 1.72 us -> 1.5 us
where the time goes in v5:
time: 80.5 us; the launch traced here: 80.4 us
  Pallas kernels  78.9 us (98%)
  local copies, waits for them, and re-layouts  1.5 us (2%)
    pallas_call x1, Pallas kernels, shards(): pl.pallas_call(kernel, name='experts', out_shape=jax.ShapeDtypeStruct((EX...  78.9 us

profile of v5, /device:TPU:1, one launch (start us, length us, event | category | flops | bytes accessed | tf_op | source)
XLA Modules:
  0.0 80.4 jit_solution(5164976611162190892)
XLA Ops:
  0.0 0.0 copy-start
  0.0 0.8 copy-done
  0.8 78.9 %experts.1 = bf16[2,80,1024]{2,1,0:T(8,128)(2,1)S(1)} custom-call(s32[2,5120]{1,0:T(2,128)S(1)} %bitcast.1, bf16[640,1536]{1,0:T(8,128)(2,1)} %tok_hbm.1, bf16[2,1536,128]{2,1,0:T(8,128)(2,1)} %wg_hbm.1, bf16[2,1536,128]{2,1,0:T(8,128)(2,1)} %wu_hbm.1), custom_call_target="tpu_custom_call" | custom-call | tf_op jit(solution)/shard_map/experts/pallas_call | solution.py:397
  79.6 0.7 copy.6
Async XLA Ops:
  0.0 0.8 copy-start

commit v6 on v5

--- a/solution.py
+++ b/solution.py
@@ -21,16 +21,16 @@
 PIECES = ((0, 1), (1, 2), (3, 1))
 
 PLAN = (
-    "w00", "r001", "r211", "r111", "r301", "w01", "r011", "r002", "r212", "r101", "r112", "r302",
-    "r012", "r003", "r311", "w10", "r102", "r113", "r201", "r013", "f01", "r004", "f00", "r312",
-    "r103", "r114", "r202", "t0", "r313", "r303", "t1", "r203", "w11", "a012", "a002", "r314",
-    "a101", "r213", "r204", "a013", "a111", "t3", "a003", "a102", "a014", "t2", "a311", "a301",
-    "f10", "f11", "a004", "a112", "a015", "q000", "q010", "a103", "a211", "a201", "k000", "k010",
-    "a312", "a302", "q001", "q011", "k001", "a113", "k011", "a104", "q020", "q021", "k020", "k021",
+    "w00", "r001", "r101", "r111", "r011", "r301", "r211", "w01", "r002", "r112", "r102", "r012",
+    "r212", "r003", "r113", "r201", "r311", "r103", "r013", "r004", "w10", "f00", "r114", "r302",
+    "r202", "r312", "t0", "t1", "f01", "r303", "r313", "r203", "a012", "r213", "a002", "a101",
+    "r314", "w11", "r204", "a013", "a003", "a111", "t3", "a102", "a014", "t2", "f10", "a004",
+    "a301", "a311", "a112", "a015", "q010", "q000", "a103", "a211", "a201", "k010", "k000", "a312",
+    "a302", "q011", "q001", "k011", "k001", "a113", "a104", "q021", "q020", "f11", "k021", "k020",
     "a212", "a202", "a313", "a303", "p1001", "p1101", "h10", "a213", "a203", "h11", "a304", "a214",
-    "p1201", "p310", "p3001", "p311", "p3201", "h12", "p2101", "p200", "p2201", "p201", "o10", "m10",
-    "o01", "m01", "o11", "o00", "m00", "m11", "o02", "m02", "b10", "o12", "m12", "b01",
-    "b11", "b00", "b02", "b12",
+    "p1201", "p310", "p3201", "h12", "p311", "p3001", "p2101", "p2201", "p2001", "o10", "m10", "o01",
+    "m01", "o02", "m02", "o11", "m11", "o00", "m00", "b10", "o12", "m12", "b01", "b02",
+    "b11", "b00", "b12",
 )
 
 
@@ -158,8 +158,7 @@
         return (col * 4 + to_hi * 2 + to_core) * BLOCK
 
     def place_rows(c):
-        if once("ids"):
-            find_ranks()
+        if once("tok"):
             tok_in.wait()
         index = lax.broadcasted_iota(jnp.int32, (BLOCK, count), 0)
         slot = jnp.concatenate([index + slot_start(c, 0), index + slot_start(c, 1)], axis=0)
@@ -379,6 +378,7 @@
         for b in positions(piece)[0]:
             out_ref[e, :, out_lanes(1 - xl, b)] = back[e, :, b * LANES : (b + 1) * LANES]
 
+    find_ranks()
     pl.semaphore_wait(barrier, len(partners))
     acts = {
         "w": send_weights, "f": pass_weights, "r": reduce_step, "t": finish_reduce, "a": gather_step,

time: 80.5 us -> 79.9 us (level)
  no operation moved by 1% of the time
where the time goes in v6:
time: 79.9 us; the launch traced here: 79.8 us
  Pallas kernels  78.3 us (98%)
  local copies, waits for them, and re-layouts  1.5 us (2%)
    pallas_call x1, Pallas kernels, shards(): pl.pallas_call(kernel, name='experts', out_shape=jax.ShapeDtypeStruct((EX...  78.3 us

profile of v6, /device:TPU:1, one launch (start us, length us, event | category | flops | bytes accessed | tf_op | source)
XLA Modules:
  0.0 79.8 jit_solution(14753757922055404746)
XLA Ops:
  0.0 0.0 copy-start
  0.0 0.8 copy-done
  0.8 78.3 %experts.1 = bf16[2,80,1024]{2,1,0:T(8,128)(2,1)S(1)} custom-call(s32[2,5120]{1,0:T(2,128)S(1)} %bitcast.1, bf16[640,1536]{1,0:T(8,128)(2,1)} %tok_hbm.1, bf16[2,1536,128]{2,1,0:T(8,128)(2,1)} %wg_hbm.1, bf16[2,1536,128]{2,1,0:T(8,128)(2,1)} %wu_hbm.1), custom_call_target="tpu_custom_call" | custom-call | tf_op jit(solution)/shard_map/experts/pallas_call | solution.py:397
  79.1 0.7 copy.6
Async XLA Ops:
  0.0 0.8 copy-start

commit v7 on v6

--- a/solution.py
+++ b/solution.py
@@ -379,6 +379,9 @@
             out_ref[e, :, out_lanes(1 - xl, b)] = back[e, :, b * LANES : (b + 1) * LANES]
 
     find_ranks()
+    for c in range(2):
+        once("p", c)
+        place_rows(c)
     pl.semaphore_wait(barrier, len(partners))
     acts = {
         "w": send_weights, "f": pass_weights, "r": reduce_step, "t": finish_reduce, "a": gather_step,

time: 79.9 us -> 79 us (0.989)
  Pallas kernels: 78.3 us -> 77.3 us
    pallas_call x1, Pallas kernels: 78.3 us -> 77.3 us  [shards(): pl.pallas_call(kernel, name='experts', out_shape=jax.ShapeDtypeStruct((EX...]
where the time goes in v7:
time: 79 us; the launch traced here: 78.9 us
  Pallas kernels  77.3 us (98%)
  local copies, waits for them, and re-layouts  1.5 us (2%)
    pallas_call x1, Pallas kernels, shards(): pl.pallas_call(kernel, name='experts', out_shape=jax.ShapeDtypeStruct((EX...  77.3 us

profile of v7, /device:TPU:1, one launch (start us, length us, event | category | flops | bytes accessed | tf_op | source)
XLA Modules:
  0.0 78.9 jit_solution(18051498697082519929)
XLA Ops:
  0.0 0.0 copy-start
  0.0 0.8 copy-done
  0.8 77.3 %experts.1 = bf16[2,80,1024]{2,1,0:T(8,128)(2,1)S(1)} custom-call(s32[2,5120]{1,0:T(2,128)S(1)} %bitcast.1, bf16[640,1536]{1,0:T(8,128)(2,1)} %tok_hbm.1, bf16[2,1536,128]{2,1,0:T(8,128)(2,1)} %wg_hbm.1, bf16[2,1536,128]{2,1,0:T(8,128)(2,1)} %wu_hbm.1), custom_call_target="tpu_custom_call" | custom-call | tf_op jit(solution)/shard_map/experts/pallas_call | solution.py:400
  78.1 0.7 copy.6
Async XLA Ops:
  0.0 0.8 copy-start
